TPU v7x, 32 devices: a whole 2x2x4 slice. The times are simulated.
32 devices in a mesh: grp: 2 (over y), reg: 4 (over z), sub: 4 (over x, core).
Axes of the slice: x: 2, y: 2, z: 4, core: 2. Of those that a mesh axis runs over, the one named last changes fastest.
Arguments:
- column_state: float32 [2, 128, 8192], P('grp', None, ('reg', 'sub')), may hold values from -6 to 6
- neighbours: int32 [2, 3, 8192], P('grp', None, ('reg', 'sub')), may hold values from 0 to 1055, as said below
- mixing: float32 [2, 128, 128], P('grp'), may hold values from -0.109375 to 0.109375
- diffusivity: float32 [2, 128], P('grp'), may hold values from 0.03 to 0.3
- flux_map: float32 [4, 128], replicated, may hold values from -0.625 to 0.625
- force_map: float32 [128, 4], replicated, may hold values from -3 to 3
- return_map: float32 [3, 128], replicated, may hold values from -0.5 to 0.5
- sources: int32 [3, 8192], P(None, ('reg', 'sub')), may hold values from 0 to 2047
- remap_weights: float32 [3, 8192], P(None, ('reg', 'sub')), may hold values from 0.1 to 0.6
- wet: int32 [8192], P(('reg', 'sub')), may hold values 0 or 1
Outputs:
- new_state: float32 [2, 128, 8192], P('grp', None, ('reg', 'sub'))
- coupled_surface: float32 [3, 8192], P(None, ('reg', 'sub'))
Inputs may be any that keep to these rules, and one draw needn't show every extreme that they name: A cell's neighbours lie within 2 rows and 2 columns of it in its extended patch. sources point into the ocean cell's own slab.
All inputs are finite; a program needn't handle non-finite values. No bound on the sum of `wet` on one device may be relied on, other than what follows from the above.
Results may differ from a plain program's by a relative error of at most 0.0001.
Values sent between devices are 32-bit elements; how exact they have to be, the bound alone decides.
No kernel may reach another device: no remote copies, remote signals or barrier semaphores. Data moves between devices by JAX's collectives and lax.ppermute only.
A program may use at most 64 MiB of HBM per device.

v0:
```python
import functools
import jax
import jax.numpy as jnp
from jax import lax
from jax.experimental import pallas as pl
from jax.experimental.pallas import tpu as pltpu
from jax.sharding import PartitionSpec as P

LA = 90
BS = 128
HALO = 2
STEPS = 4
RIM = HALO * STEPS
TAPS = 2 * HALO + 1
HIGH = lax.Precision.HIGHEST
F32 = jnp.float32
BF16 = jnp.bfloat16
LANES = 128
WIDE = 2 * LANES


def up8(n):
    return -(-n // 8) * 8


def dot(a, b):
    return jnp.dot(a, b, precision=HIGH, preferred_element_type=F32)


def lane_of(width=LANES, rows=8):
    return lax.broadcasted_iota(jnp.int32, (rows, width), 1)


def roll(x, shift):
    shift = shift % x.shape[1]
    return x if shift == 0 else pltpu.roll(x, shift, 1)


def call(body, outs, *args, scratch=(), vmem=None, flops=100000, space=pltpu.VMEM):
    size = sum(a.size * a.dtype.itemsize for a in args)
    return pl.pallas_call(
        body,
        out_shape=outs,
        in_specs=[pl.BlockSpec(memory_space=space) for _ in args],
        out_specs=jax.tree.map(lambda _: pl.BlockSpec(memory_space=pltpu.VMEM), outs),
        scratch_shapes=list(scratch),
        compiler_params=pltpu.CompilerParams(vmem_limit_bytes=vmem),
        cost_estimate=pl.CostEstimate(flops=flops, bytes_accessed=size, transcendentals=0),
    )(*args)


def shape(*dims, dtype=F32):
    return jax.ShapeDtypeStruct(dims, dtype)


def pack_body(links, state, cell_in, xin, to_left, to_right, table):
    levels, cells = xin.shape
    rows = cells // BS
    ocean = lax.axis_index("grp") == 1

    @pl.when(jnp.logical_not(ocean))
    def _():
        level = lax.broadcasted_iota(jnp.int32, (levels, cells), 0)
        xin[...] = jnp.where(level < LA, state[...], 0.0)
        xin[LA : LA + links, :] = cell_in[0:links, :]

    @pl.when(ocean)
    def _():
        xin[...] = state[...]

    lane = lane_of()
    quarter = levels // 4
    span = rows * RIM
    for g in range(quarter // 8):
        left = jnp.zeros((8, LANES), F32)
        right = jnp.zeros((8, LANES), F32)
        for q in range(4):
            for i in range(rows):
                at = q * span + i * RIM
                here = (lane >= at) & (lane < at + RIM)
                block = xin[q * quarter + 8 * g : q * quarter + 8 * g + 8, i * BS : (i + 1) * BS]
                left = jnp.where(here, roll(block, at), left)
                right = jnp.where(here, roll(block, at - (BS - RIM)), right)
        to_left[8 * g : 8 * g + 8, :] = left
        to_right[8 * g : 8 * g + 8, :] = right
    table[...] = cell_in[links : links + 8, :]
    for c in range(cells // LANES):
        part = table[:, c * LANES : (c + 1) * LANES]
        to_left[quarter + 8 * c : quarter + 8 * c + 8, :] = part
        to_right[quarter + 8 * c : quarter + 8 * c + 8, :] = part


def level_matrix(mixing):
    levels = mixing.shape[0]
    row = lax.broadcasted_iota(jnp.int32, (levels, levels), 0)
    col = lax.broadcasted_iota(jnp.int32, (levels, levels), 1)
    full = mixing[...] + jnp.where(row == col, 1.0, 0.0)
    return full, jnp.where((row < LA) & (col < LA), full, 0.0)


def fields_body(nf, nr, links, mixing, small, fields, face0):
    levels = mixing.shape[0]
    full, base = level_matrix(mixing)
    r = small[0:1, :]
    ocean = lax.axis_index("grp") == 1
    at = nf * STEPS
    fields[...] = jnp.zeros(fields.shape, F32)

    @pl.when(jnp.logical_not(ocean))
    def _():
        pair = jnp.concatenate([base * (1.0 - float(links) * r), base * r], axis=1)
        lead = jnp.concatenate([small[1 : 1 + nf, :], jnp.zeros((8 - nf, levels), F32)], axis=0)
        have = [lead]
        total = [jnp.zeros((8, levels), F32) for _ in range(STEPS + 1)]
        for n in range(1, STEPS + 1):
            out = dot(jnp.concatenate(have, axis=0) if len(have) > 1 else have[0], pair)
            new = []
            for j in range(n + 1):
                term = jnp.zeros((8, levels), F32)
                if j < n:
                    term = term + out[8 * j : 8 * j + 8, :levels]
                if j > 0:
                    term = term + out[8 * j - 8 : 8 * j, levels:]
                new.append(term)
                total[j] = total[j] + term
            have = new
        for j in range(STEPS + 1):
            to = nf * ((j - 1) % (STEPS + 1))
            fields[to : to + nf, :] = total[j][0:nf, :] * (1.0 / STEPS)
        k = lax.broadcasted_iota(jnp.int32, (links, levels), 0)
        c = lax.broadcasted_iota(jnp.int32, (links, levels), 1)
        fields[at + nf : at + nf + links, :] = jnp.where(c == LA + k, 1.0, 0.0)
        face0[...] = jnp.zeros(face0.shape, F32)

    @pl.when(ocean)
    def _():
        first = 1 + 2 * nf
        lead = jnp.concatenate(
            [small[first : first + nr, :], jnp.zeros((8 - nr, levels), F32)], axis=0
        )
        through = dot(lead, full)
        face0[...] = through * (1.0 - float(links) * r)
        fields[at : at + nr, :] = (through * r)[0:nr, :]


def powers_body(nf, nr, links, mixing, small, powers, own_mix, lift):
    levels = mixing.shape[0]
    full, base = level_matrix(mixing)
    r = small[0:1, :]
    ocean = lax.axis_index("grp") == 1

    @pl.when(jnp.logical_not(ocean))
    def _():
        def squared(mats):
            n = len(mats)
            prod = dot(jnp.concatenate(mats, axis=0), jnp.concatenate(mats, axis=1))
            outs = []
            for j in range(2 * n - 1):
                term = None
                for a in range(n):
                    b = j - a
                    if 0 <= b < n:
                        piece = prod[a * levels : (a + 1) * levels, b * levels : (b + 1) * levels]
                        term = piece if term is None else term + piece
                outs.append(term)
            return outs

        mats = squared(squared([base * (1.0 - float(links) * r), base * r]))
        keep = powers.shape[0]
        for j in range(STEPS + 1):
            powers[:, j * levels : (j + 1) * levels] = mats[j][0:keep, :]

    @pl.when(ocean)
    def _():
        own_mix[:, 0:levels] = full * (1.0 - float(links) * r)
        own_mix[:, levels : 2 * levels] = full * r
        first = 1 + 2 * nf
        lead = jnp.concatenate(
            [small[first : first + nr, :], jnp.zeros((8 - nr, levels), F32)], axis=0
        )
        top = jnp.concatenate(
            [small[1 + nf : 1 + 2 * nf, :], jnp.zeros((8 - nf, levels), F32)], axis=0
        )
        lifted = lax.dot_general(
            full, top, (((1,), (1,)), ((), ())), precision=HIGH, preferred_element_type=F32
        )
        lift[0:levels, :] = lifted
        lift[levels : levels + 8, :] = dot(lead, lifted)


def side_body(xin, from_right, from_left, fields, face0, up, dn, ext, q0, side_levels):
    levels, cells = xin.shape
    rows = cells // BS
    quarter, half = levels // 4, levels // 2
    span = rows * RIM
    lane = lane_of()
    ocean = lax.axis_index("grp") == 1
    sent = up.shape[0] - half * LANES // cells
    edge = HALO * BS
    for g in range(levels // 8):
        q, at = (8 * g) // quarter, (8 * g) % quarter
        a = roll(from_right[at : at + 8, :], -span * q)
        b = roll(from_left[at : at + 8, :], span - span * q)
        side_levels[8 * g : 8 * g + 8, :] = jnp.where(
            lane < span, a, jnp.where(lane < 2 * span, b, 0.0)
        )
    both = jnp.concatenate([fields[...], face0[...]], axis=0)
    full = dot(both, xin[...])
    n = fields.shape[0]
    ext[:, 0:cells] = full[0:n, :]
    q0[...] = full[n : n + 8, :]
    ext[:, cells : cells + LANES] = dot(fields[...], side_levels[...])
    for g in range(half // 8):
        low = side_levels[8 * g : 8 * g + 8, :]
        high = side_levels[half + 8 * g : half + 8 * g + 8, :]
        at, lanes = side_spot(sent, half, cells, 8 * g)
        both = low + roll(high, 2 * span)
        up[at : at + 8, lanes] = both
        dn[at : at + 8, lanes] = both

    @pl.when(jnp.logical_not(ocean))
    def _():
        up[0:sent, :] = xin[0:sent, :]
        dn[0:sent, :] = xin[0:sent, :]

    @pl.when(ocean)
    def _():
        for part in range(2):
            rows_of = slice(part * half, (part + 1) * half)
            lanes_of = slice(part * edge, (part + 1) * edge)
            up[0:half, lanes_of] = xin[rows_of, cells - edge : cells]
            dn[0:half, lanes_of] = xin[rows_of, 0:edge]
        up[half:sent, :] = jnp.zeros((sent - half, cells), F32)
        dn[half:sent, :] = jnp.zeros((sent - half, cells), F32)


def side_spot(sent, half, cells, gs):
    rows = half * LANES // cells
    c, at = divmod(gs, rows)
    return sent + at, slice(c * LANES, (c + 1) * LANES)


def side_lanes(block, at_right, at_left):
    lane = lane_of()
    a = roll(block, -at_right)
    b = roll(block, LANES - RIM - at_left)
    return jnp.where(lane < RIM, a, jnp.where(lane >= LANES - RIM, b, 0.0))


def place_row(x_ref, i, at, blocks, rows):
    span = rows * RIM
    for g, (main, side, shift) in enumerate(blocks):
        x_ref[8 * g : 8 * g + 8, at * WIDE : at * WIDE + LANES] = main
        x_ref[8 * g : 8 * g + 8, at * WIDE + LANES : (at + 1) * WIDE] = side_lanes(
            side, shift + i * RIM, shift + span + i * RIM
        )


def tap_counts(codes, coef, rows, first_row, links):
    count, wide = codes.shape[1], codes.shape[2]
    row = (lax.broadcasted_iota(jnp.int32, (count, wide), 0) + first_row) % rows
    pcol = lax.broadcasted_iota(jnp.int32, (count, wide), 1) % LANES
    width = BS + 2 * HALO
    kinds = []
    for k in range(links):
        n = codes[k].astype(jnp.int32)
        line = ((n.astype(F32) + 0.5) * (1.0 / width)).astype(jnp.int32)
        kinds.append((line - row) * 16 + (n - line * width - pcol))
    for dr in range(TAPS):
        for dc in range(TAPS):
            hits = jnp.zeros((count, wide), F32)
            for k in range(links):
                hits = hits + jnp.where(kinds[k] == dr * 16 + dc, 1.0, 0.0)
            coef[dr * TAPS + dc] = roll(hits, dc - HALO)


def stencil(src, dst, coef, groups, first, count, batch, step=1):
    def row(i):
        off = [pl.multiple_of((i + dr - HALO) * WIDE, WIDE) for dr in range(TAPS)]
        here = pl.multiple_of(i * WIDE, WIDE)
        for g0 in range(0, groups, batch):
            gs = range(g0, min(g0 + batch, groups))
            acc = {}
            for dr in range(TAPS):
                v = {g: src[8 * g : 8 * g + 8, pl.ds(off[dr], WIDE)] for g in gs}
                for dc in range(TAPS):
                    c = coef[dr * TAPS + dc, pl.ds(i, 1), :]
                    for g in gs:
                        t = c * v[g]
                        acc[g, dc] = t if dr == 0 else acc[g, dc] + t
            for g in gs:
                total = acc[g, HALO]
                for dc in range(TAPS):
                    if dc != HALO:
                        total = total + roll(acc[g, dc], HALO - dc)
                dst[8 * g : 8 * g + 8, pl.ds(here, WIDE)] = total

    def one(o, _):
        for p in range(step):
            row(first + o * step + p)
        return 0

    lax.fori_loop(0, count // step, one, 0)


def chain(xa, xb, coef, groups, rows, near, batch, take, step=1):
    total = rows * (2 * near + 1)
    refs = (xa, xb)
    lo = near * rows
    take(0, xa, lo)
    for j in range(1, STEPS + 1):
        src, dst = refs[(j - 1) % 2], refs[j % 2]
        first = lo - RIM + HALO * j
        stencil(src, dst, coef, groups, first, total - 2 * first, batch, step)
        take(j, dst, lo)


def ext_row(block, g, i, rows):
    cells = rows * BS
    main = block[8 * g : 8 * g + 8, i * BS : (i + 1) * BS]
    side = side_lanes(block[8 * g : 8 * g + 8, cells : cells + LANES], i * RIM, (rows + i) * RIM)
    return main, side


def flux_body(rows, near, nf, links, *refs):
    n = 2 * near + 1
    blocks, (mine, q0, cell_in, out, xa, xb, codes, coef, ua, ub, own_codes, own_coef) = (
        refs[:n], refs[n:],
    )
    cells = rows * BS
    groups = nf * STEPS // 8

    @pl.when(lax.axis_index("grp") == 1)
    def _():
        codes[...] = jnp.zeros(codes.shape, F32)
        own_codes[...] = jnp.zeros(own_codes.shape, F32)
        for d in range(n):
            for i in range(rows):
                at = d * rows + i
                for g in range(groups):
                    main, side = ext_row(blocks[d], g, i, rows)
                    xa[8 * g : 8 * g + 8, at * WIDE : at * WIDE + LANES] = main
                    xa[8 * g : 8 * g + 8, at * WIDE + LANES : (at + 1) * WIDE] = side
                main, side = ext_row(blocks[d], groups, i, rows)
                for k in range(links):
                    codes[k, at : at + 1, 0:LANES] = main[nf + k : nf + k + 1, :]
                    codes[k, at : at + 1, LANES:WIDE] = side[nf + k : nf + k + 1, :]
                to = at - near * rows + HALO
                if 0 <= to < rows + 2 * HALO:
                    if d == near:
                        main, side = ext_row(mine, groups, i, rows)
                        for k in range(links):
                            own_codes[k, to : to + 1, 0:LANES] = cell_in[
                                k : k + 1, i * BS : (i + 1) * BS
                            ]
                    ua[:, to * WIDE : to * WIDE + LANES] = main
                    ua[:, to * WIDE + LANES : (to + 1) * WIDE] = side
        tap_counts(own_codes, own_coef, rows, rows - HALO, links)
        stencil(ua, ub, own_coef, 1, HALO, rows, 1, rows)
        tap_counts(codes, coef, rows, 0, links)
        own = blocks[near]
        out[0:nf, :] = own[nf * STEPS : nf * (STEPS + 1), 0:cells]
        for i in range(rows):
            here = slice(i * BS, (i + 1) * BS)
            face = q0[:, here] + ub[:, (HALO + i) * WIDE : (HALO + i) * WIDE + LANES]
            out[nf:8, here] = face[0 : 8 - nf, :]

        def take(j, ref, lo):
            if j == 0:
                return
            at = nf * (j - 1)
            for i in range(rows):
                here = slice(i * BS, (i + 1) * BS)
                out[0:nf, here] = (
                    out[0:nf, here] + ref[at : at + nf, (lo + i) * WIDE : (lo + i) * WIDE + LANES]
                )

        chain(xa, xb, coef, groups, rows, near, groups, take, 4)


def ocean_body(rows, links, sent, xin, cell_in, above, below, own, near, x, y, codes, coef):
    levels, cells = xin.shape
    half, edge = levels // 2, HALO * BS
    groups = levels // 8

    @pl.when(lax.axis_index("grp") == 1)
    def _():
        for at in range(rows + 2 * HALO):
            if at < HALO:
                i, side = rows - HALO + at, above
            elif at < HALO + rows:
                i, side = at - HALO, own
            else:
                i, side = at - HALO - rows, below
            parts = []
            for g in range(groups):
                part, gs = divmod(8 * g, half)
                if at < HALO:
                    main = above[gs : gs + 8, part * edge + at * BS : part * edge + (at + 1) * BS]
                elif at < HALO + rows:
                    main = xin[8 * g : 8 * g + 8, i * BS : (i + 1) * BS]
                else:
                    main = below[gs : gs + 8, part * edge + i * BS : part * edge + (i + 1) * BS]
                s, lanes = side_spot(sent, half, cells, gs)
                parts.append((main, side[s : s + 8, lanes], part * 2 * rows * RIM))
            place_row(x, i, at, parts, rows)
        codes[...] = jnp.zeros(codes.shape, F32)
        for k in range(links):
            for i in range(rows):
                codes[k, HALO + i : HALO + i + 1, 0:LANES] = cell_in[
                    k : k + 1, i * BS : (i + 1) * BS
                ]
        tap_counts(codes, coef, rows, rows - HALO, links)
        stencil(x, y, coef, groups, HALO, rows, 3)
        for i in range(rows):
            near[:, i * BS : (i + 1) * BS] = y[:, (HALO + i) * WIDE : (HALO + i) * WIDE + LANES]


def onto_body(links, cells, count, *refs):
    tables, (high, low, whole) = refs[:count], refs[count:]
    me = lax.axis_index("sub")
    for d in range(count):
        at = pl.multiple_of(((me + d) % count) * cells, cells)
        if tables[d].shape[1] == cells:
            whole[:, pl.ds(at, cells)] = tables[d][...]
        else:
            first = tables[d].shape[0] - 8 * (cells // LANES)
            for c in range(cells // LANES):
                whole[:, pl.ds(pl.multiple_of(at + c * LANES, LANES), LANES)] = tables[d][
                    first + 8 * c : first + 8 * c + 8, :
                ]

    @pl.when(lax.axis_index("grp") == 1)
    def _():
        def chunk(c, _):
            at = pl.multiple_of(c * LANES, LANES)
            src = whole[0:links, pl.ds(at, LANES)].astype(jnp.int32) - me * cells
            w = whole[links : 2 * links, pl.ds(at, LANES)]
            for t in range(0, cells, 16):
                target = lax.broadcasted_iota(jnp.int32, (16, LANES), 0) + t
                value = jnp.zeros((16, LANES), F32)
                for k in range(links):
                    value = value + jnp.where(src[k : k + 1, :] == target, w[k : k + 1, :], 0.0)
                top = value.astype(BF16)
                high[t : t + 16, pl.ds(at, LANES)] = top
                low[t : t + 16, pl.ds(at, LANES)] = (value - top.astype(F32)).astype(BF16)
            return 0

        lax.fori_loop(0, count * cells // LANES, chunk, 0)


def stacked(x, y):
    sub = lax.broadcasted_iota(jnp.int32, x.shape, 0)
    return jnp.where(sub < 4, x, pltpu.roll(y, 4, 0))


def couple_body(links, nf, nr, count, *refs):
    blocks, (whole, high, low, lift, own_flux, out, slab, pair, surface) = (
        refs[:count], refs[count:],
    )
    cells = blocks[0].shape[1]
    levels = lift.shape[0] - 8
    me = lax.axis_index("sub")

    @pl.when(lax.axis_index("grp") == 1)
    def _():
        for d in range(count):
            at = pl.multiple_of(((me + d) % count) * cells, cells)
            block = blocks[d][...]
            slab[:, pl.ds(at, cells)] = block
            pair[:, pl.ds(at, cells)] = stacked(block, block)
        chunks = count * cells // LANES
        half = chunks // 2
        per = min(chunks, 16)
        mine = cells // LANES
        sub = lax.broadcasted_iota(jnp.int32, (8, LANES), 0)

        def two(a, b):
            return jnp.where(sub < 4, a, b)

        def target(c):
            at0 = pl.multiple_of(c * LANES, LANES)
            at1 = pl.multiple_of((c + half) * LANES, LANES)
            t0, t1 = whole[:, pl.ds(at0, LANES)], whole[:, pl.ds(at1, LANES)]
            src, w = [], []
            for k in range(links):
                src.append(two(t0[k : k + 1, :], t1[k : k + 1, :]).astype(jnp.int32))
                w.append(two(t0[links + k : links + k + 1, :], t1[links + k : links + k + 1, :]))
            lanes = [x & (LANES - 1) for x in src]
            homes = [x // LANES for x in src]

            def source(o, acc):
                acc = list(acc)
                for p in range(per):
                    b = o * per + p
                    v = pair[:, pl.ds(pl.multiple_of(b * LANES, LANES), LANES)]
                    for k in range(links):
                        got = jnp.take_along_axis(v, lanes[k], axis=1)
                        acc[k] = jnp.where(homes[k] == b, got, acc[k])
                return tuple(acc)

            zero = tuple(jnp.zeros((8, LANES), F32) for _ in range(links))
            got = source(0, zero) if chunks == per else lax.fori_loop(0, chunks // per, source, zero)
            flux = w[0] * got[0]
            for k in range(1, links):
                flux = flux + w[k] * got[k]
            s0, s1 = slab[:, pl.ds(at0, LANES)], slab[:, pl.ds(at1, LANES)]
            face = stacked(pltpu.roll(s0, 8 - nf, 0), pltpu.roll(s1, 8 - nf, 0))
            col = lift[levels : levels + 8, :]
            col = stacked(col, col)
            for f in range(nf):
                face = face + col[:, f : f + 1] * two(flux[f : f + 1, :], flux[4 + f : 5 + f, :])
            n = 2 * links
            face = jnp.where(
                sub % 4 < nr, face * two(t0[n : n + 1, :], t1[n : n + 1, :]), 0.0
            )
            surface[:, pl.ds(at0, LANES)] = face
            for part, lift_rows in ((0, flux), (1, pltpu.roll(flux, 4, 0))):
                here = c + part * half - me * mine

                @pl.when((here >= 0) & (here < mine))
                def _():
                    own_flux[:, pl.ds(pl.multiple_of(here * LANES, LANES), LANES)] = jnp.where(
                        sub < nf, lift_rows, 0.0
                    )

        def some(o, _):
            for p in range(2):
                target(o * 2 + p)
            return 0

        lax.fori_loop(0, half // 2, some, 0)
        face = surface[...]
        top = face.astype(BF16)
        rest = (face - top.astype(F32)).astype(BF16)
        both = jnp.concatenate([top, rest], axis=0)

        def nt(a, b):
            return lax.dot_general(a, b, (((1,), (1,)), ((), ())), preferred_element_type=F32)

        cut = half * LANES
        one = nt(both, high[:, 0:cut])
        two_ = nt(top, low[:, 0:cut])
        three = nt(both, high[:, cut : 2 * cut])
        four = nt(top, low[:, cut : 2 * cut])
        first = one[0:8, :] + one[8:16, :] + two_
        second = three[0:8, :] + three[8:16, :] + four
        out[...] = first + pltpu.roll(second, 4, 0)


def place_blocks(x, codes, blocks, spots, sent, half, links):
    rows = blocks[0].shape[1] // BS
    for block, at0 in zip(blocks, spots):
        for i in range(rows):
            parts = []
            for g in range(sent // 8):
                part, gs = divmod(8 * g, half)
                s, lanes = side_spot(sent, half, block.shape[1], gs)
                parts.append(
                    (
                        block[8 * g : 8 * g + 8, i * BS : (i + 1) * BS],
                        block[s : s + 8, lanes],
                        part * 2 * rows * RIM,
                    )
                )
            at = at0 + i
            place_row(x, i, at, parts, rows)
            for k in range(links):
                s = LA + k
                codes[k, at : at + 1, :] = x[s : s + 1, at * WIDE : (at + 1) * WIDE]


def inner_body(rows, links, sent, levels, above, own, below, x0, x1, x2, codes, coef):
    groups = sent // 8
    total = 3 * rows

    @pl.when(lax.axis_index("grp") == 0)
    def _():
        codes[...] = jnp.zeros(codes.shape, F32)
        place_blocks(
            x0, codes, (above, own, below), (0, rows, 2 * rows), sent, levels // 2, links
        )
        tap_counts(codes, coef, rows, 0, links)
        stencil(x0, x1, coef, groups, HALO, total - 2 * HALO, 3)
        stencil(x1, x2, coef, groups, 2 * HALO, total - 4 * HALO, 3)


def state_body(rows, links, sent, far_up, far_dn, x0_in, x1_in, x2_in, powers, xin, near_sum,
               own_mix, own_flux, lift, table, out, x0, x1, x2, x3, codes, coef, basis):
    levels, cells = out.shape
    groups = sent // 8
    total = 5 * rows
    ocean = lax.axis_index("grp") == 1

    @pl.when(ocean)
    def _():
        start = xin[...]
        now = (
            dot(own_mix[:, 0:levels], start)
            + dot(own_mix[:, levels:], near_sum[...])
            + dot(lift[0:levels, :], own_flux[...])
        )
        wet = table[2 * links : 2 * links + 1, :]
        out[...] = start + wet * (now - start)

    @pl.when(jnp.logical_not(ocean))
    def _():
        codes[...] = jnp.zeros(codes.shape, F32)
        for j, (ref, given) in enumerate(((x0, x0_in), (x1, x1_in), (x2, x2_in))):
            lo, hi = HALO * j, 3 * rows - HALO * j
            ref[:, (rows + lo) * WIDE : (rows + hi) * WIDE] = given[:, lo * WIDE : hi * WIDE]
        place_blocks(
            x0, codes, (far_up, far_dn), (0, 4 * rows), sent, levels // 2, links
        )
        for at in range(rows, 4 * rows):
            for k in range(links):
                s = LA + k
                codes[k, at : at + 1, :] = x0[s : s + 1, at * WIDE : (at + 1) * WIDE]
        tap_counts(codes, coef, rows, 0, links)

        def apply(src, dst, j, done=None):
            lo, hi = HALO * j, total - HALO * j
            if done is None:
                stencil(src, dst, coef, groups, lo, hi - lo, 3)
                return
            stencil(src, dst, coef, groups, lo, done[0] - lo, 3)
            stencil(src, dst, coef, groups, done[1], hi - done[1], 3)

        apply(x0, x1, 1, (rows + HALO, 4 * rows - HALO))
        apply(x1, x2, 2, (rows + 2 * HALO, 4 * rows - 2 * HALO))
        apply(x2, x3, 3)
        basis[...] = jnp.zeros(basis.shape, F32)
        mid = 2 * rows

        def take(j, ref):
            for i in range(rows):
                basis[j * levels : j * levels + sent, i * BS : (i + 1) * BS] = ref[
                    0:sent, (mid + i) * WIDE : (mid + i) * WIDE + LANES
                ]

        for j, ref in enumerate((x0, x1, x2, x3)):
            take(j, ref)
        apply(x3, x0, 4)
        take(4, x0)
        out[0:sent, :] = dot(powers[...], basis[...])
        if sent < levels:
            out[sent:levels, :] = jnp.zeros((levels - sent, cells), F32)


def local(
    column_state,
    neighbours,
    mixing,
    diffusivity,
    flux_map,
    force_map,
    return_map,
    sources,
    remap_weights,
    wet,
):
    levels, cells = column_state.shape[1:]
    rows = cells // BS
    links = neighbours.shape[1]
    nf, nr = flux_map.shape[0], return_map.shape[0]
    near = -(-RIM // rows)
    n = 2 * near + 1
    sent = max(up8(LA + links), levels // 2)
    n_reg, n_sub = lax.axis_size("reg"), lax.axis_size("sub")
    axes = ("grp", "reg", "sub")

    def at(g, r, s):
        return (g * n_reg + r % n_reg) * n_sub + s % n_sub

    spots = [(r, s) for r in range(n_reg) for s in range(n_sub)]

    def shift(x, axis, d):
        size = lax.axis_size(axis)
        return lax.ppermute(x, axis, [((i + d) % size, i) for i in range(size)])

    def stack_rows(parts, count):
        out, at = None, 0
        for p in parts:
            here = jnp.pad(p, ((at, up8(count) - at - p.shape[0]), (0, 0)))
            at += p.shape[0]
            out = here if out is None else out + here
        return out

    whole_numbers = stack_rows(
        [neighbours[0], sources, jnp.zeros((links, cells), jnp.int32), wet[None]], 3 * links + 2
    )
    cell_in = whole_numbers.astype(F32) + jnp.pad(
        remap_weights, ((2 * links, up8(3 * links + 2) - 3 * links), (0, 0))
    )
    small = stack_rows([diffusivity, flux_map, force_map.T, return_map], 1 + 2 * nf + nr)
    ext_rows = up8(nf * (STEPS + 1) + links)
    message = levels // 4 + 8 * (cells // LANES)
    xin, to_left, to_right, table = call(
        functools.partial(pack_body, links),
        (
            shape(levels, cells),
            shape(message, LANES),
            shape(message, LANES),
            shape(8, cells),
        ),
        column_state[0], cell_in,
        vmem=8 << 20,
    )
    from_right = shift(to_left, "sub", 1)
    from_left = shift(to_right, "sub", -1)
    fields, face0 = call(
        functools.partial(fields_body, nf, nr, links),
        (shape(ext_rows, levels), shape(8, levels)),
        mixing[0], small,
        vmem=8 << 20,
    )
    powers, own_mix, lift = call(
        functools.partial(powers_body, nf, nr, links),
        (
            shape(sent, (STEPS + 1) * levels),
            shape(levels, 2 * levels),
            shape(levels + 8, 8),
        ),
        mixing[0], small,
        vmem=8 << 20,
    )
    block = sent + levels // 2 * LANES // cells
    up, dn, ext, q0 = call(
        side_body,
        (
            shape(block, cells),
            shape(block, cells),
            shape(ext_rows, cells + LANES),
            shape(8, cells),
        ),
        xin, from_right, from_left, fields, face0,
        scratch=[pltpu.VMEM((levels, LANES), F32)],
        vmem=8 << 20,
    )

    hop = lax.ppermute(ext, axes, [(at(0, r, s), at(1, r, s)) for r, s in spots])
    line = lax.broadcasted_iota(jnp.int32, ext.shape, 0)
    relay = jnp.where((line >= nf * STEPS) & (line < nf * (STEPS + 1)), ext, hop)
    got, mains = {0: hop}, {}
    for d in sorted(range(-near, near + 1), key=abs):
        key = d % n_reg
        if key in got:
            continue
        pairs = [(at(1, r + d, s), at(1, r, s)) for r, s in spots]
        got[key] = lax.ppermute(relay, axes, pairs)
        groups = (0, 1) if abs(d) == 1 else (0,)
        pairs = [(at(g, r + d, s), at(g, r, s)) for g in groups for r, s in spots]
        mains[key] = lax.ppermute(up if d < 0 else dn, axes, pairs)
    ext_blocks = [got[d % n_reg] for d in range(-near, near + 1)]
    above, below = mains[-1 % n_reg], mains[1 % n_reg]

    tables = [table] + [None] * (n_sub - 1)
    tables[1], tables[n_sub - 1] = from_right, from_left
    for d in range(2, n_sub - 1):
        tables[d] = shift(table, "sub", d)
    span = n_sub * cells
    high, low, whole = call(
        functools.partial(onto_body, links, cells, n_sub),
        (shape(cells, span, dtype=BF16), shape(cells, span, dtype=BF16), shape(8, span)),
        *tables,
        vmem=24 << 20,
    )

    ext_o = up8(rows + 2 * HALO)
    near_sum = call(
        functools.partial(ocean_body, rows, links, sent),
        shape(levels, cells),
        xin, cell_in, above, below, up,
        scratch=[
            pltpu.VMEM((levels, (rows + 2 * HALO) * WIDE), F32),
            pltpu.VMEM((levels, (rows + 2 * HALO) * WIDE), F32),
            pltpu.VMEM((links, ext_o, WIDE), F32),
            pltpu.VMEM((TAPS * TAPS, ext_o, WIDE), F32),
        ],
        vmem=16 << 20,
    )

    total = rows * n
    ext_n = up8(total)
    fq = call(
        functools.partial(flux_body, rows, near, nf, links),
        shape(8, cells),
        *ext_blocks, ext, q0, cell_in,
        scratch=[
            pltpu.VMEM((nf * STEPS, total * WIDE), F32),
            pltpu.VMEM((nf * STEPS, total * WIDE), F32),
            pltpu.VMEM((links, ext_n, WIDE), F32),
            pltpu.VMEM((TAPS * TAPS, ext_n, WIDE), F32),
            pltpu.VMEM((8, (rows + 2 * HALO) * WIDE), F32),
            pltpu.VMEM((8, (rows + 2 * HALO) * WIDE), F32),
            pltpu.VMEM((links, ext_o, WIDE), F32),
            pltpu.VMEM((TAPS * TAPS, ext_o, WIDE), F32),
        ],
        vmem=8 << 20,
    )
    blocks = [fq] + [shift(fq, "sub", d) for d in range(1, n_sub)]
    own_flux, coupled = call(
        functools.partial(couple_body, links, nf, nr, n_sub),
        (shape(8, cells), shape(8, cells)),
        *blocks, whole, high, low, lift,
        scratch=[
            pltpu.VMEM((8, span), F32),
            pltpu.VMEM((8, span), F32),
            pltpu.VMEM((8, span // 2), F32),
        ],
        vmem=24 << 20,
    )
    back = lax.ppermute(coupled, axes, [(at(1, r, s), at(0, r, s)) for r, s in spots])

    wide = 3 * rows * WIDE
    ext_i = up8(3 * rows)
    x0, x1, x2 = call(
        functools.partial(inner_body, rows, links, sent, levels),
        (shape(sent, wide), shape(sent, wide), shape(sent, wide)),
        above, up, below,
        scratch=[
            pltpu.VMEM((links, ext_i, WIDE), F32),
            pltpu.VMEM((TAPS * TAPS, ext_i, WIDE), F32),
        ],
        vmem=12 << 20,
    )
    new_state = call(
        functools.partial(state_body, rows, links, sent),
        shape(levels, cells),
        mains[-2 % n_reg], mains[2 % n_reg], x0, x1, x2, powers, xin, near_sum, own_mix, own_flux,
        lift, table,
        scratch=[pltpu.VMEM((sent, total * WIDE), F32) for _ in range(4)]
        + [
            pltpu.VMEM((links, ext_n, WIDE), F32),
            pltpu.VMEM((TAPS * TAPS, ext_n, WIDE), F32),
            pltpu.VMEM(((STEPS + 1) * levels, cells), F32),
        ],
        vmem=24 << 20,
    )
    ocean_side = lax.axis_index("grp") == 1
    surface = jnp.where(ocean_side, coupled[:nr], back[:nr])
    return (new_state[None], surface)


def solution(mesh):
    in_specs = (
        P("grp", None, ("reg", "sub")),
        P("grp", None, ("reg", "sub")),
        P("grp", None, None),
        P("grp", None),
        P(),
        P(),
        P(),
        P(None, ("reg", "sub")),
        P(None, ("reg", "sub")),
        P(("reg", "sub")),
    )
    out_specs = (P("grp", None, ("reg", "sub")), P(None, ("reg", "sub")))
    return jax.shard_map(local, mesh=mesh, in_specs=in_specs, out_specs=out_specs, check_vma=False)
```

profile of v0, /device:TPU:0, one launch (start us, length us, event | category | flops | bytes accessed | tf_op | source)
XLA Modules:
  0.0 57.3 jit_solution(7814475744465188555)
XLA Ops:
  0.6 0.7 %copy.14 = s32[1,3,512]{2,1,0:T(4,128)S(1)} copy(s32[1,3,512]{2,0,1:T(1,128)} %param.11) | data formatting | bytes 12288
  1.4 0.1 pad.40
  1.4 0.8 %pad_add_fusion.cell_in.refs_7_ = f32[16,512]{1,0:T(8,128)S(1)} fusion(f32[3,512]{1,0:T(4,128)} %param.18, s32[1,512]{1,0:T(1,128)} %bitcast.14, s32[3,512]{1,0:T(4,128)} %param.17, s32[3,512]{1,0:T(4,128)S(1)} %bitcast.12, s32[16]{0:T(128)S(1)} %pad.40), kind=kLoop, calls=%fused_computation | loop fusion | flops 40960 | bytes 53312 | tf_op jit(solution)/shard_map/add | solution.py:692
  2.3 0.9 %copy-done = f32[1,128,512]{2,1,0:T(8,128)S(1)} copy-done((f32[1,128,512]{2,1,0:T(8,128)S(1)}, f32[1,128,512]{2,1,0:T(8,128)}, u32[]{:S(2)}) %copy-start) | copy-done | bytes 262168
  3.2 0.2 shard_map.113
  3.4 2.5 %collective-permute-start = (f32[64,128]{1,0:T(8,128)S(1)}, f32[64,128]{1,0:T(8,128)S(1)}, u32[]{:S(2)}, u32[]{:S(2)}) collective-permute-start(f32[64,128]{1,0:T(8,128)S(1)} %get-tuple-element.24), channel_id=1, source_target_pairs={{1,0},{2,1},{3,2},{0,3},{5,4},{6,5},{7,6},{4,7},{9,8},{10,9},{11,1... | collective-permute-start | bytes 98312 | tf_op jit(solution)/shard_map/ppermute | solution.py:679
  5.9 0.7 %pad_add_fusion.1.small = f32[16,128]{1,0:T(8,128)S(1)} fusion(f32[3,128]{1,0:T(4,128)} %param.16, f32[4,128]{1,0:T(4,128)} %bitcast.13, f32[4,128]{1,0:T(4,128)} %param.14, f32[1,128]{1,0:T(1,128)} %param.13), kind=kLoop, calls=%fused_computation.4 | loop fusion | flops 6144 | bytes 14336 | tf_op jit(solution)/shard_map/add | solution.py:686
  6.6 0.8 %copy-done.1 = f32[1,128,128]{2,1,0:T(8,128)S(1)} copy-done((f32[1,128,128]{2,1,0:T(8,128)S(1)}, f32[1,128,128]{2,1,0:T(8,128)}, u32[]{:S(2)}) %copy-start.1) | copy-done | bytes 65560
  7.4 0.8 %shard_map.114 = (f32[24,128]{1,0:T(8,128)S(1)}, f32[8,128]{1,0:T(8,128)S(1)}) custom-call(f32[128,128]{1,0:T(8,128)S(1)} %bitcast.9, f32[16,128]{1,0:T(8,128)S(1)} %pad_add_fusion.1.small), custom_call_target="tpu_custom_call" | custom-call | flops 100000 | bytes 73728 | tf_op jit(solution)/shard_map/pallas_call | solution.py:41
  8.3 0.9 %collective-permute-done.1.from_left.refs_3_ = f32[64,128]{1,0:T(8,128)S(1)} collective-permute-done((f32[64,128]{1,0:T(8,128)S(1)}, f32[64,128]{1,0:T(8,128)S(1)}, u32[]{:S(2)}, u32[]{:S(2)}) %collective-permute-start.1) | collective-permute-done | bytes 32800 | tf_op jit(solution)/shard_map/ppermute | solution.py:679
  9.2 0.3 shard_map.115
  9.5 3.5 %collective-permute-start.5 = (f32[24,640]{1,0:T(8,128)S(1)}, f32[24,640]{1,0:T(8,128)S(1)}, u32[]{:S(2)}, u32[]{:S(2)}) collective-permute-start(f32[24,640]{1,0:T(8,128)S(1)} %get-tuple-element.35.refs_5_), channel_id=1, source_target_pairs={{0,16},{1,17},{2,18},{3,19},{4,20},{5,21},{6,22},{7,23},{8,24},{9,... | collective-permute-start | bytes 184328 | tf_op jit(solution)/shard_map/ppermute | solution.py:741
  13.0 1.8 %collective-permute-done.5.refs_2_ = f32[24,640]{1,0:T(8,128)S(1)} collective-permute-done((f32[24,640]{1,0:T(8,128)S(1)}, f32[24,640]{1,0:T(8,128)S(1)}, u32[]{:S(2)}, u32[]{:S(2)}) %collective-permute-start.5) | collective-permute-done | bytes 61472 | tf_op jit(solution)/shard_map/ppermute | solution.py:741
  14.8 0.1 broadcast_select_fusion
  14.9 0.7 %collective-permute-start.6 = (f32[24,640]{1,0:T(8,128)S(1)}, f32[24,640]{1,0:T(8,128)S(1)}, u32[]{:S(2)}, u32[]{:S(2)}) collective-permute-start(f32[24,640]{1,0:T(8,128)S(1)} %broadcast_select_fusion), channel_id=1, source_target_pairs={{24,16},{25,17},{26,18},{27,19},{28,20},{29,21},{30,22},{31,23},{1... | collective-permute-start | bytes 184328 | tf_op jit(solution)/shard_map/ppermute | solution.py:750
  15.6 0.7 %collective-permute-start.7 = (f32[24,640]{1,0:T(8,128)S(1)}, f32[24,640]{1,0:T(8,128)S(1)}, u32[]{:S(2)}, u32[]{:S(2)}) collective-permute-start(f32[24,640]{1,0:T(8,128)S(1)} %broadcast_select_fusion), channel_id=1, source_target_pairs={{28,16},{29,17},{30,18},{31,19},{16,20},{17,21},{18,22},{19,23},{2... | collective-permute-start | bytes 184328 | tf_op jit(solution)/shard_map/ppermute | solution.py:750
  16.2 0.7 %collective-permute-start.8 = (f32[24,640]{1,0:T(8,128)S(1)}, f32[24,640]{1,0:T(8,128)S(1)}, u32[]{:S(2)}, u32[]{:S(2)}) collective-permute-start(f32[24,640]{1,0:T(8,128)S(1)} %broadcast_select_fusion), channel_id=1, source_target_pairs={{20,16},{21,17},{22,18},{23,19},{24,20},{25,21},{26,22},{27,23},{2... | collective-permute-start | bytes 184328 | tf_op jit(solution)/shard_map/ppermute | solution.py:750
  16.9 1.0 %collective-permute-start.12 = (f32[8,512]{1,0:T(8,128)S(1)}, f32[8,512]{1,0:T(8,128)S(1)}, u32[]{:S(2)}, u32[]{:S(2)}) collective-permute-start(f32[8,512]{1,0:T(8,128)S(1)} %get-tuple-element.37.refs_0_.table), channel_id=1, source_target_pairs={{2,0},{3,1},{0,2},{1,3},{6,4},{7,5},{4,6},{5,7},{10,8},{11,9},{8,1... | collective-permute-start | bytes 49160 | tf_op jit(solution)/shard_map/ppermute | solution.py:679
  17.9 1.2 %collective-permute-start.10 = (f32[8,512]{1,0:T(8,128)S(1)}, f32[8,512]{1,0:T(8,128)S(1)}, u32[]{:S(2)}, u32[]{:S(2)}) collective-permute-start(f32[8,512]{1,0:T(8,128)S(1)} %shard_map.119.refs_0_), channel_id=1, source_target_pairs={{2,0},{3,1},{0,2},{1,3},{6,4},{7,5},{4,6},{5,7},{10,8},{11,9},{8,1... | collective-permute-start | bytes 49160 | tf_op jit(solution)/shard_map/ppermute | solution.py:679
  19.1 1.7 %collective-permute-start.9 = (f32[8,512]{1,0:T(8,128)S(1)}, f32[8,512]{1,0:T(8,128)S(1)}, u32[]{:S(2)}, u32[]{:S(2)}) collective-permute-start(f32[8,512]{1,0:T(8,128)S(1)} %shard_map.119.refs_0_), channel_id=1, source_target_pairs={{1,0},{2,1},{3,2},{0,3},{5,4},{6,5},{7,6},{4,7},{9,8},{10,9},{11,1... | collective-permute-start | bytes 49160 | tf_op jit(solution)/shard_map/ppermute | solution.py:679
  20.8 1.3 %shard_map.117 = (f32[96,640]{1,0:T(8,128)S(1)}, f32[128,256]{1,0:T(8,128)S(1)}, f32[136,8]{1,0:T(8,128)S(1)}) custom-call(f32[128,128]{1,0:T(8,128)S(1)} %bitcast.10, f32[16,128]{1,0:T(8,128)S(1)} %pad_add_fusion.1.small), custom_call_target="tpu_custom_call" | custom-call | flops 100000 | bytes 73728 | tf_op jit(solution)/shard_map/pallas_call | solution.py:41
  22.2 0.1 collective-permute-done.11.refs_3_
  22.3 0.0 collective-permute-done.9.refs_1_
  22.3 1.3 %collective-permute-start.13 = (f32[8,512]{1,0:T(8,128)S(1)}, f32[8,512]{1,0:T(8,128)S(1)}, u32[]{:S(2)}, u32[]{:S(2)}) collective-permute-start(f32[8,512]{1,0:T(8,128)S(1)} %get-tuple-element.43), channel_id=1, source_target_pairs={{16,0},{17,1},{18,2},{19,3},{20,4},{21,5},{22,6},{23,7},{24,8},{25... | collective-permute-start | bytes 49160 | tf_op jit(solution)/shard_map/ppermute | solution.py:813
  23.6 1.6 %collective-permute-start.3 = (f32[112,512]{1,0:T(8,128)S(1)}, f32[112,512]{1,0:T(8,128)S(1)}, u32[]{:S(2)}, u32[]{:S(2)}) collective-permute-start(f32[112,512]{1,0:T(8,128)S(1)} %get-tuple-element.28.own), channel_id=1, source_target_pairs={{12,0},{13,1},{14,2},{15,3},{0,4},{1,5},{2,6},{3,7},{4,8},{5,9},{6... | collective-permute-start | bytes 688136 | tf_op jit(solution)/shard_map/ppermute | solution.py:753
  25.2 2.2 %collective-permute-start.4 = (f32[112,512]{1,0:T(8,128)S(1)}, f32[112,512]{1,0:T(8,128)S(1)}, u32[]{:S(2)}, u32[]{:S(2)}) collective-permute-start(f32[112,512]{1,0:T(8,128)S(1)} %get-tuple-element.29), channel_id=1, source_target_pairs={{4,0},{5,1},{6,2},{7,3},{8,4},{9,5},{10,6},{11,7},{12,8},{13,9},{1... | collective-permute-start | bytes 688136 | tf_op jit(solution)/shard_map/ppermute | solution.py:753
  27.5 2.7 %collective-permute-start.2 = (f32[112,512]{1,0:T(8,128)S(1)}, f32[112,512]{1,0:T(8,128)S(1)}, u32[]{:S(2)}, u32[]{:S(2)}) collective-permute-start(f32[112,512]{1,0:T(8,128)S(1)} %get-tuple-element.28.own), channel_id=1, source_target_pairs={{8,0},{9,1},{10,2},{11,3},{12,4},{13,5},{14,6},{15,7},{0,8},{1,9},... | collective-permute-start | bytes 688136 | tf_op jit(solution)/shard_map/ppermute | solution.py:753
  30.2 14.3 %collective-permute-done.13 = f32[8,512]{1,0:T(8,128)S(1)} collective-permute-done((f32[8,512]{1,0:T(8,128)S(1)}, f32[8,512]{1,0:T(8,128)S(1)}, u32[]{:S(2)}, u32[]{:S(2)}) %collective-permute-start.13) | collective-permute-done | bytes 16416 | tf_op jit(solution)/shard_map/ppermute | solution.py:813
  44.5 0.6 %slice_select_fusion = f32[3,512]{1,0:T(4,128)} fusion(f32[8,512]{1,0:T(8,128)S(1)} %collective-permute-done.13, f32[8,512]{1,0:T(8,128)S(1)} %get-tuple-element.43, pred[]{:T(512)S(6)} %eq.3), kind=kLoop, calls=%fused_computation.2 | loop fusion | flops 1536 | bytes 18433 | tf_op jit(solution)/shard_map/jit(_where)/select_n | solution.py:841
  45.1 3.3 %shard_map.116 = (f32[96,3072]{1,0:T(8,128)S(1)}, f32[96,3072]{1,0:T(8,128)S(1)}, f32[96,3072]{1,0:T(8,128)S(1)}) custom-call(f32[112,512]{1,0:T(8,128)S(1)} %collective-permute-done.3.above, f32[112,512]{1,0:T(8,128)S(1)} %get-tuple-element.28.own, f32[112,512]{1,0:T(8,128)S(1)} %collective-permute-done.4.below), custom_call_target="tpu_custom_call" | custom-call | flops 100000 | bytes 688128 | tf_op jit(solution)/shard_map/pallas_call | solution.py:41
  48.4 0.3 collective-permute-done.2.far_up.far_dn
  48.7 8.6 %shard_map.122 = f32[128,512]{1,0:T(8,128)} custom-call(f32[112,512]{1,0:T(8,128)S(1)} %collective-permute-done.2.far_up.far_dn, f32[112,512]{1,0:T(8,128)S(1)} %collective-permute-done.2.far_up.far_dn, f32[96,3072]{1,0:T(8,128)S(1)} %get-tuple-element.30.x0_in, f32[96,3072]{1,0:T(8,128)S(1)} %get-tuple-element.31.x1_in, ...), custom_call_target="tpu_custom_call" | custom-call | flops 100000 | bytes 4935936 | tf_op jit(solution)/shard_map/pallas_call | solution.py:41
  (20 shorter events, 0.1 us)
Async XLA Ops:
  0.6 20.2 %copy-start.2 = (f32[1,128,128]{2,1,0:T(8,128)S(1)}, f32[1,128,128]{2,1,0:T(8,128)}, u32[]{:S(2)}) copy-start(f32[1,128,128]{2,1,0:T(8,128)} %param.12) | copy-start | bytes 196612
  2.3 0.9 %copy-start = (f32[1,128,512]{2,1,0:T(8,128)S(1)}, f32[1,128,512]{2,1,0:T(8,128)}, u32[]{:S(2)}) copy-start(f32[1,128,512]{2,1,0:T(8,128)} %param.10) | copy-start | bytes 786436
  3.4 4.9 %collective-permute-start = (f32[64,128]{1,0:T(8,128)S(1)}, f32[64,128]{1,0:T(8,128)S(1)}, u32[]{:S(2)}, u32[]{:S(2)}) collective-permute-start(f32[64,128]{1,0:T(8,128)S(1)} %get-tuple-element.24), channel_id=1, source_target_pairs={{1,0},{2,1},{3,2},{0,3},{5,4},{6,5},{7,6},{4,7},{9,8},{10,9},{11,1... | collective-permute-start | bytes 98312 | tf_op jit(solution)/shard_map/ppermute | solution.py:679
  5.9 3.3 %collective-permute-start.1 = (f32[64,128]{1,0:T(8,128)S(1)}, f32[64,128]{1,0:T(8,128)S(1)}, u32[]{:S(2)}, u32[]{:S(2)}) collective-permute-start(f32[64,128]{1,0:T(8,128)S(1)} %get-tuple-element.25), channel_id=1, source_target_pairs={{3,0},{0,1},{1,2},{2,3},{7,4},{4,5},{5,6},{6,7},{11,8},{8,9},{9,10... | collective-permute-start | bytes 98312 | tf_op jit(solution)/shard_map/ppermute | solution.py:679
  6.6 0.8 %copy-start.1 = (f32[1,128,128]{2,1,0:T(8,128)S(1)}, f32[1,128,128]{2,1,0:T(8,128)}, u32[]{:S(2)}) copy-start(f32[1,128,128]{2,1,0:T(8,128)} %param.12) | copy-start | bytes 196612
  9.5 5.3 %collective-permute-start.5 = (f32[24,640]{1,0:T(8,128)S(1)}, f32[24,640]{1,0:T(8,128)S(1)}, u32[]{:S(2)}, u32[]{:S(2)}) collective-permute-start(f32[24,640]{1,0:T(8,128)S(1)} %get-tuple-element.35.refs_5_), channel_id=1, source_target_pairs={{0,16},{1,17},{2,18},{3,19},{4,20},{5,21},{6,22},{7,23},{8,24},{9,... | collective-permute-start | bytes 184328 | tf_op jit(solution)/shard_map/ppermute | solution.py:741
  14.9 3.0 %collective-permute-start.6 = (f32[24,640]{1,0:T(8,128)S(1)}, f32[24,640]{1,0:T(8,128)S(1)}, u32[]{:S(2)}, u32[]{:S(2)}) collective-permute-start(f32[24,640]{1,0:T(8,128)S(1)} %broadcast_select_fusion), channel_id=1, source_target_pairs={{24,16},{25,17},{26,18},{27,19},{28,20},{29,21},{30,22},{31,23},{1... | collective-permute-start | bytes 184328 | tf_op jit(solution)/shard_map/ppermute | solution.py:750
  15.6 2.3 %collective-permute-start.7 = (f32[24,640]{1,0:T(8,128)S(1)}, f32[24,640]{1,0:T(8,128)S(1)}, u32[]{:S(2)}, u32[]{:S(2)}) collective-permute-start(f32[24,640]{1,0:T(8,128)S(1)} %broadcast_select_fusion), channel_id=1, source_target_pairs={{28,16},{29,17},{30,18},{31,19},{16,20},{17,21},{18,22},{19,23},{2... | collective-permute-start | bytes 184328 | tf_op jit(solution)/shard_map/ppermute | solution.py:750
  16.2 1.7 %collective-permute-start.8 = (f32[24,640]{1,0:T(8,128)S(1)}, f32[24,640]{1,0:T(8,128)S(1)}, u32[]{:S(2)}, u32[]{:S(2)}) collective-permute-start(f32[24,640]{1,0:T(8,128)S(1)} %broadcast_select_fusion), channel_id=1, source_target_pairs={{20,16},{21,17},{22,18},{23,19},{24,20},{25,21},{26,22},{27,23},{2... | collective-permute-start | bytes 184328 | tf_op jit(solution)/shard_map/ppermute | solution.py:750
  16.9 5.2 %collective-permute-start.12 = (f32[8,512]{1,0:T(8,128)S(1)}, f32[8,512]{1,0:T(8,128)S(1)}, u32[]{:S(2)}, u32[]{:S(2)}) collective-permute-start(f32[8,512]{1,0:T(8,128)S(1)} %get-tuple-element.37.refs_0_.table), channel_id=1, source_target_pairs={{2,0},{3,1},{0,2},{1,3},{6,4},{7,5},{4,6},{5,7},{10,8},{11,9},{8,1... | collective-permute-start | bytes 49160 | tf_op jit(solution)/shard_map/ppermute | solution.py:679
  17.9 4.2 %collective-permute-start.10 = (f32[8,512]{1,0:T(8,128)S(1)}, f32[8,512]{1,0:T(8,128)S(1)}, u32[]{:S(2)}, u32[]{:S(2)}) collective-permute-start(f32[8,512]{1,0:T(8,128)S(1)} %shard_map.119.refs_0_), channel_id=1, source_target_pairs={{2,0},{3,1},{0,2},{1,3},{6,4},{7,5},{4,6},{5,7},{10,8},{11,9},{8,1... | collective-permute-start | bytes 49160 | tf_op jit(solution)/shard_map/ppermute | solution.py:679
  19.1 3.2 %collective-permute-start.11 = (f32[8,512]{1,0:T(8,128)S(1)}, f32[8,512]{1,0:T(8,128)S(1)}, u32[]{:S(2)}, u32[]{:S(2)}) collective-permute-start(f32[8,512]{1,0:T(8,128)S(1)} %shard_map.119.refs_0_), channel_id=1, source_target_pairs={{3,0},{0,1},{1,2},{2,3},{7,4},{4,5},{5,6},{6,7},{11,8},{8,9},{9,10... | collective-permute-start | bytes 49160 | tf_op jit(solution)/shard_map/ppermute | solution.py:679
  19.1 3.2 %collective-permute-start.9 = (f32[8,512]{1,0:T(8,128)S(1)}, f32[8,512]{1,0:T(8,128)S(1)}, u32[]{:S(2)}, u32[]{:S(2)}) collective-permute-start(f32[8,512]{1,0:T(8,128)S(1)} %shard_map.119.refs_0_), channel_id=1, source_target_pairs={{1,0},{2,1},{3,2},{0,3},{5,4},{6,5},{7,6},{4,7},{9,8},{10,9},{11,1... | collective-permute-start | bytes 49160 | tf_op jit(solution)/shard_map/ppermute | solution.py:679
  22.3 22.2 %collective-permute-start.13 = (f32[8,512]{1,0:T(8,128)S(1)}, f32[8,512]{1,0:T(8,128)S(1)}, u32[]{:S(2)}, u32[]{:S(2)}) collective-permute-start(f32[8,512]{1,0:T(8,128)S(1)} %get-tuple-element.43), channel_id=1, source_target_pairs={{16,0},{17,1},{18,2},{19,3},{20,4},{21,5},{22,6},{23,7},{24,8},{25... | collective-permute-start | bytes 49160 | tf_op jit(solution)/shard_map/ppermute | solution.py:813
  23.6 21.5 %collective-permute-start.3 = (f32[112,512]{1,0:T(8,128)S(1)}, f32[112,512]{1,0:T(8,128)S(1)}, u32[]{:S(2)}, u32[]{:S(2)}) collective-permute-start(f32[112,512]{1,0:T(8,128)S(1)} %get-tuple-element.28.own), channel_id=1, source_target_pairs={{12,0},{13,1},{14,2},{15,3},{0,4},{1,5},{2,6},{3,7},{4,8},{5,9},{6... | collective-permute-start | bytes 688136 | tf_op jit(solution)/shard_map/ppermute | solution.py:753
  25.2 19.9 %collective-permute-start.4 = (f32[112,512]{1,0:T(8,128)S(1)}, f32[112,512]{1,0:T(8,128)S(1)}, u32[]{:S(2)}, u32[]{:S(2)}) collective-permute-start(f32[112,512]{1,0:T(8,128)S(1)} %get-tuple-element.29), channel_id=1, source_target_pairs={{4,0},{5,1},{6,2},{7,3},{8,4},{9,5},{10,6},{11,7},{12,8},{13,9},{1... | collective-permute-start | bytes 688136 | tf_op jit(solution)/shard_map/ppermute | solution.py:753
  27.5 21.2 %collective-permute-start.2 = (f32[112,512]{1,0:T(8,128)S(1)}, f32[112,512]{1,0:T(8,128)S(1)}, u32[]{:S(2)}, u32[]{:S(2)}) collective-permute-start(f32[112,512]{1,0:T(8,128)S(1)} %get-tuple-element.28.own), channel_id=1, source_target_pairs={{8,0},{9,1},{10,2},{11,3},{12,4},{13,5},{14,6},{15,7},{0,8},{1,9},... | collective-permute-start | bytes 688136 | tf_op jit(solution)/shard_map/ppermute | solution.py:753
where the time goes:
time: 57.7 us; the launch traced here: 57.3 us
  starting transfers between devices  19.7 us (34%)
  waiting for transfers between devices  17.5 us (30%)
  Pallas kernels  14.5 us (25%)
  local copies, waits for them, and re-layouts  2.59 us (4%)
  other arithmetic  2.21 us (4%)
  between operations  0.79 us (1%)
    pallas_call x10, Pallas kernels, call(): pl.pallas_call(body, out_shape=outs, in_specs=[pl.BlockSpec(memory_space=...  14.5 us
    ppermute x1, waiting for transfers between devices, local(): lax.ppermute(coupled, axes, [(at(1, r, s), at(0, r, s)) for r, s in spots])  14.3 us
    ppermute x3, starting transfers between devices, local(): mains[key] = lax.ppermute(up if d < 0 else dn, axes, pairs)  6.56 us
    ppermute x6, starting transfers between devices, shift(): return lax.ppermute(x, axis, [((i + d) % size, i) for i in range(size)])  6.36 us
    ppermute x1, starting transfers between devices, local(): lax.ppermute(ext, axes, [(at(0, r, s), at(1, r, s)) for r, s in spots])  3.46 us
    unnamed x7, local copies, waits for them, and re-layouts  2.52 us
    ppermute x3, starting transfers between devices, local(): got[key] = lax.ppermute(relay, axes, pairs)  1.98 us
    ppermute x1, waiting for transfers between devices, local(): lax.ppermute(ext, axes, [(at(0, r, s), at(1, r, s)) for r, s in spots])  1.83 us
  transfers between devices with their start and end apart: 14, of which 5 were waited for; matrix products, arithmetic and copies ran while one was open for 2% of the time, Pallas kernels for 10%

commit v1 on v0

--- a/solution.py
+++ b/solution.py
@@ -36,14 +36,15 @@
     return x if shift == 0 else pltpu.roll(x, shift, 1)
 
 
-def call(body, outs, *args, scratch=(), vmem=None, flops=100000, space=pltpu.VMEM):
+def call(body, outs, *args, scratch=(), vmem=None, flops=100000, alias=None):
     size = sum(a.size * a.dtype.itemsize for a in args)
     return pl.pallas_call(
         body,
         out_shape=outs,
-        in_specs=[pl.BlockSpec(memory_space=space) for _ in args],
+        in_specs=[pl.BlockSpec(memory_space=pltpu.VMEM) for _ in args],
         out_specs=jax.tree.map(lambda _: pl.BlockSpec(memory_space=pltpu.VMEM), outs),
         scratch_shapes=list(scratch),
+        input_output_aliases=alias or {},
         compiler_params=pltpu.CompilerParams(vmem_limit_bytes=vmem),
         cost_estimate=pl.CostEstimate(flops=flops, bytes_accessed=size, transcendentals=0),
     )(*args)
@@ -143,7 +144,7 @@
         fields[at : at + nr, :] = (through * r)[0:nr, :]
 
 
-def powers_body(nf, nr, links, mixing, small, powers, own_mix, lift):
+def powers_body(nf, nr, links, sent, mixing, small, powers, own_mix, lift):
     levels = mixing.shape[0]
     full, base = level_matrix(mixing)
     r = small[0:1, :]
@@ -166,9 +167,16 @@
             return outs
 
         mats = squared(squared([base * (1.0 - float(links) * r), base * r]))
-        keep = powers.shape[0]
+        wide = powers.shape[1]
+        whole = jnp.zeros((sent, wide), F32)
         for j in range(STEPS + 1):
-            powers[:, j * levels : (j + 1) * levels] = mats[j][0:keep, :]
+            part = jnp.concatenate(
+                [mats[j][0:sent, :], jnp.zeros((sent, wide - levels), F32)], axis=1
+            )
+            whole = whole + roll(part, j * sent)
+        top = whole.astype(BF16)
+        powers[0:sent, :] = top
+        powers[sent : 2 * sent, :] = (whole - top.astype(F32)).astype(BF16)
 
     @pl.when(ocean)
     def _():
@@ -188,14 +196,14 @@
         lift[levels : levels + 8, :] = dot(lead, lifted)
 
 
-def side_body(xin, from_right, from_left, fields, face0, up, dn, ext, q0, side_levels):
+def side_body(xin, from_right, from_left, fields, face0, up, dn, far, ext, q0, extra, side_levels):
     levels, cells = xin.shape
     rows = cells // BS
     quarter, half = levels // 4, levels // 2
     span = rows * RIM
     lane = lane_of()
     ocean = lax.axis_index("grp") == 1
-    sent = up.shape[0] - half * LANES // cells
+    sent = up.shape[0]
     edge = HALO * BS
     for g in range(levels // 8):
         q, at = (8 * g) // quarter, (8 * g) % quarter
@@ -213,15 +221,21 @@
     for g in range(half // 8):
         low = side_levels[8 * g : 8 * g + 8, :]
         high = side_levels[half + 8 * g : half + 8 * g + 8, :]
-        at, lanes = side_spot(sent, half, cells, 8 * g)
         both = low + roll(high, 2 * span)
-        up[at : at + 8, lanes] = both
-        dn[at : at + 8, lanes] = both
+        at, lanes = side_spot(0, half, cells, 8 * g)
+        extra[at : at + 8, lanes] = both
+
+    n = half * LANES // cells
+    more = extra.shape[0] - n
+    extra[n:, 0:cells] = xin[sent : sent + more, :]
+    extra[:, cells:] = jnp.zeros((n + more, LANES), F32)
 
     @pl.when(jnp.logical_not(ocean))
     def _():
-        up[0:sent, :] = xin[0:sent, :]
-        dn[0:sent, :] = xin[0:sent, :]
+        up[...] = xin[0:sent, :]
+        dn[...] = xin[0:sent, :]
+        far[0:sent, :] = xin[0:sent, :]
+        far[sent:, :] = extra[:, 0:cells]
 
     @pl.when(ocean)
     def _():
@@ -230,8 +244,9 @@
             lanes_of = slice(part * edge, (part + 1) * edge)
             up[0:half, lanes_of] = xin[rows_of, cells - edge : cells]
             dn[0:half, lanes_of] = xin[rows_of, 0:edge]
-        up[half:sent, :] = jnp.zeros((sent - half, cells), F32)
-        dn[half:sent, :] = jnp.zeros((sent - half, cells), F32)
+        for ref in (up, dn):
+            ref[half : half + n, :] = extra[0:n, 0:cells]
+            ref[half + n :, :] = jnp.zeros((sent - half - n, cells), F32)
 
 
 def side_spot(sent, half, cells, gs):
@@ -256,14 +271,14 @@
         )
 
 
-def tap_counts(codes, coef, rows, first_row, links):
-    count, wide = codes.shape[1], codes.shape[2]
+def tap_counts(codes, coef, rows, first_row, links, at=0, count=None):
+    count, wide = count or codes.shape[1], codes.shape[2]
     row = (lax.broadcasted_iota(jnp.int32, (count, wide), 0) + first_row) % rows
     pcol = lax.broadcasted_iota(jnp.int32, (count, wide), 1) % LANES
     width = BS + 2 * HALO
     kinds = []
     for k in range(links):
-        n = codes[k].astype(jnp.int32)
+        n = codes[k, at : at + count, :].astype(jnp.int32)
         line = ((n.astype(F32) + 0.5) * (1.0 / width)).astype(jnp.int32)
         kinds.append((line - row) * 16 + (n - line * width - pcol))
     for dr in range(TAPS):
@@ -271,10 +286,14 @@
             hits = jnp.zeros((count, wide), F32)
             for k in range(links):
                 hits = hits + jnp.where(kinds[k] == dr * 16 + dc, 1.0, 0.0)
-            coef[dr * TAPS + dc] = roll(hits, dc - HALO)
-
-
-def stencil(src, dst, coef, groups, first, count, batch, step=1):
+            coef[dr * TAPS + dc, at : at + count, :] = roll(hits, dc - HALO)
+
+
+def same(i):
+    return i
+
+
+def stencil(src, dst, coef, groups, first, count, batch, step=1, slot=same):
     def row(i):
         off = [pl.multiple_of((i + dr - HALO) * WIDE, WIDE) for dr in range(TAPS)]
         here = pl.multiple_of(i * WIDE, WIDE)
@@ -284,7 +303,7 @@
             for dr in range(TAPS):
                 v = {g: src[8 * g : 8 * g + 8, pl.ds(off[dr], WIDE)] for g in gs}
                 for dc in range(TAPS):
-                    c = coef[dr * TAPS + dc, pl.ds(i, 1), :]
+                    c = coef[dr * TAPS + dc, pl.ds(slot(i), 1), :]
                     for g in gs:
                         t = c * v[g]
                         acc[g, dc] = t if dr == 0 else acc[g, dc] + t
@@ -378,7 +397,7 @@
         chain(xa, xb, coef, groups, rows, near, groups, take, 4)
 
 
-def ocean_body(rows, links, sent, xin, cell_in, above, below, own, near, x, y, codes, coef):
+def ocean_body(rows, links, xin, cell_in, above, below, own, near, x, y, codes, coef):
     levels, cells = xin.shape
     half, edge = levels // 2, HALO * BS
     groups = levels // 8
@@ -401,7 +420,7 @@
                     main = xin[8 * g : 8 * g + 8, i * BS : (i + 1) * BS]
                 else:
                     main = below[gs : gs + 8, part * edge + i * BS : part * edge + (i + 1) * BS]
-                s, lanes = side_spot(sent, half, cells, gs)
+                s, lanes = side_spot(half, half, cells, gs)
                 parts.append((main, side[s : s + 8, lanes], part * 2 * rows * RIM))
             place_row(x, i, at, parts, rows)
         codes[...] = jnp.zeros(codes.shape, F32)
@@ -548,49 +567,70 @@
         out[...] = first + pltpu.roll(second, 4, 0)
 
 
-def place_blocks(x, codes, blocks, spots, sent, half, links):
-    rows = blocks[0].shape[1] // BS
-    for block, at0 in zip(blocks, spots):
-        for i in range(rows):
-            parts = []
-            for g in range(sent // 8):
-                part, gs = divmod(8 * g, half)
-                s, lanes = side_spot(sent, half, block.shape[1], gs)
-                parts.append(
-                    (
-                        block[8 * g : 8 * g + 8, i * BS : (i + 1) * BS],
-                        block[s : s + 8, lanes],
-                        part * 2 * rows * RIM,
-                    )
-                )
-            at = at0 + i
-            place_row(x, i, at, parts, rows)
-            for k in range(links):
-                s = LA + k
-                codes[k, at : at + 1, :] = x[s : s + 1, at * WIDE : (at + 1) * WIDE]
-
-
-def inner_body(rows, links, sent, levels, above, own, below, x0, x1, x2, codes, coef):
+def place_block(x, codes, block, extra, keep, base, b, sent, half, links):
+    rows = block.shape[1] // BS
+    for i in range(rows):
+        parts = []
+        for g in range(sent // 8):
+            part, gs = divmod(8 * g, half)
+            s, lanes = side_spot(0, half, block.shape[1], gs)
+            here = slice(i * BS, (i + 1) * BS)
+            over = 8 * g - keep
+            if over < 0:
+                main = block[8 * g : 8 * g + 8, here]
+            else:
+                over += base + half * LANES // block.shape[1]
+                main = extra[over : over + 8, here]
+            parts.append((main, extra[base + s : base + s + 8, lanes], part * 2 * rows * RIM))
+        at = b * rows + i
+        place_row(x, i, at, parts, rows)
+        for k in range(links):
+            s = LA + k
+            codes[k, 8 * b + i : 8 * b + i + 1, :] = x[s : s + 1, at * WIDE : (at + 1) * WIDE]
+
+
+def slot_of(rows):
+    return lambda i: i + (i // rows) * (8 - rows)
+
+
+def split_rows(high, low, j, ref, first, rows, sent):
+    for i in range(rows):
+        value = ref[0:sent, (first + i) * WIDE : (first + i) * WIDE + LANES]
+        top = value.astype(BF16)
+        here = slice(i * BS, (i + 1) * BS)
+        high[j * sent : (j + 1) * sent, here] = top
+        low[j * sent : (j + 1) * sent, here] = (value - top.astype(F32)).astype(BF16)
+
+
+def inner_body(rows, links, sent, levels, above, own, below, more_above, more, more_below, x0, x1, x2, coef, high, low, codes):
     groups = sent // 8
-    total = 3 * rows
+    slot = slot_of(rows)
+    lo, hi, mid = rows, 4 * rows, 2 * rows
 
     @pl.when(lax.axis_index("grp") == 0)
     def _():
         codes[...] = jnp.zeros(codes.shape, F32)
-        place_blocks(
-            x0, codes, (above, own, below), (0, rows, 2 * rows), sent, levels // 2, links
-        )
-        tap_counts(codes, coef, rows, 0, links)
-        stencil(x0, x1, coef, groups, HALO, total - 2 * HALO, 3)
-        stencil(x1, x2, coef, groups, 2 * HALO, total - 4 * HALO, 3)
-
-
-def state_body(rows, links, sent, far_up, far_dn, x0_in, x1_in, x2_in, powers, xin, near_sum,
-               own_mix, own_flux, lift, table, out, x0, x1, x2, x3, codes, coef, basis):
+        for b, block, extra in ((1, above, more_above), (2, own, more), (3, below, more_below)):
+            place_block(
+                x0, codes, block, extra, block.shape[0], 0, b, sent, levels // 2, links
+            )
+        tap_counts(codes, coef, 8, 0, links, 8, 24)
+        stencil(x0, x1, coef, groups, lo + HALO, hi - lo - 2 * HALO, 3, 1, slot)
+        stencil(x1, x2, coef, groups, lo + 2 * HALO, hi - lo - 4 * HALO, 3, 1, slot)
+        used = (STEPS + 1) * sent
+        high[used:, :] = jnp.zeros((high.shape[0] - used, high.shape[1]), BF16)
+        low[used:, :] = jnp.zeros((high.shape[0] - used, high.shape[1]), BF16)
+        for j, ref in enumerate((x0, x1, x2)):
+            split_rows(high, low, j, ref, mid, rows, sent)
+
+
+def state_body(rows, links, sent, keep, far_up, far_dn, x0_, x1_, x2_, coef_, high_, low_, powers, xin,
+               near_sum, own_mix, own_flux, lift, table, out, x0, x1, x2, coef, high, low, x3, codes):
     levels, cells = out.shape
     groups = sent // 8
     total = 5 * rows
     ocean = lax.axis_index("grp") == 1
+    slot = slot_of(rows)
 
     @pl.when(ocean)
     def _():
@@ -606,43 +646,33 @@
     @pl.when(jnp.logical_not(ocean))
     def _():
         codes[...] = jnp.zeros(codes.shape, F32)
-        for j, (ref, given) in enumerate(((x0, x0_in), (x1, x1_in), (x2, x2_in))):
-            lo, hi = HALO * j, 3 * rows - HALO * j
-            ref[:, (rows + lo) * WIDE : (rows + hi) * WIDE] = given[:, lo * WIDE : hi * WIDE]
-        place_blocks(
-            x0, codes, (far_up, far_dn), (0, 4 * rows), sent, levels // 2, links
-        )
-        for at in range(rows, 4 * rows):
-            for k in range(links):
-                s = LA + k
-                codes[k, at : at + 1, :] = x0[s : s + 1, at * WIDE : (at + 1) * WIDE]
-        tap_counts(codes, coef, rows, 0, links)
+        for b, block in ((0, far_up), (4, far_dn)):
+            place_block(x0, codes, block, block, keep, keep, b, sent, levels // 2, links)
+            tap_counts(codes, coef, 8, 0, links, 8 * b, 8)
 
         def apply(src, dst, j, done=None):
             lo, hi = HALO * j, total - HALO * j
             if done is None:
-                stencil(src, dst, coef, groups, lo, hi - lo, 3)
+                stencil(src, dst, coef, groups, lo, hi - lo, 3, 1, slot)
                 return
-            stencil(src, dst, coef, groups, lo, done[0] - lo, 3)
-            stencil(src, dst, coef, groups, done[1], hi - done[1], 3)
-
+            stencil(src, dst, coef, groups, lo, done[0] - lo, 3, 1, slot)
+            stencil(src, dst, coef, groups, done[1], hi - done[1], 3, 1, slot)
+
+        mid = 2 * rows
         apply(x0, x1, 1, (rows + HALO, 4 * rows - HALO))
         apply(x1, x2, 2, (rows + 2 * HALO, 4 * rows - 2 * HALO))
         apply(x2, x3, 3)
-        basis[...] = jnp.zeros(basis.shape, F32)
-        mid = 2 * rows
-
-        def take(j, ref):
-            for i in range(rows):
-                basis[j * levels : j * levels + sent, i * BS : (i + 1) * BS] = ref[
-                    0:sent, (mid + i) * WIDE : (mid + i) * WIDE + LANES
-                ]
-
-        for j, ref in enumerate((x0, x1, x2, x3)):
-            take(j, ref)
+        split_rows(high, low, 3, x3, mid, rows, sent)
         apply(x3, x0, 4)
-        take(4, x0)
-        out[0:sent, :] = dot(powers[...], basis[...])
+        split_rows(high, low, 4, x0, mid, rows, sent)
+        top = powers[...]
+
+        def mm(a, b):
+            return jnp.dot(a, b, preferred_element_type=F32)
+
+        one = mm(top, high[...])
+        two = mm(top[0:sent, :], low[...])
+        out[0:sent, :] = one[0:sent, :] + one[sent : 2 * sent, :] + two
         if sent < levels:
             out[sent:levels, :] = jnp.zeros((levels - sent, cells), F32)
 
@@ -694,6 +724,7 @@
     )
     small = stack_rows([diffusivity, flux_map, force_map.T, return_map], 1 + 2 * nf + nr)
     ext_rows = up8(nf * (STEPS + 1) + links)
+    packed = -(-(STEPS + 1) * sent // LANES) * LANES
     message = levels // 4 + 8 * (cells // LANES)
     xin, to_left, to_right, table = call(
         functools.partial(pack_body, links),
@@ -715,42 +746,48 @@
         vmem=8 << 20,
     )
     powers, own_mix, lift = call(
-        functools.partial(powers_body, nf, nr, links),
+        functools.partial(powers_body, nf, nr, links, sent),
         (
-            shape(sent, (STEPS + 1) * levels),
+            shape(2 * sent, packed, dtype=BF16),
             shape(levels, 2 * levels),
             shape(levels + 8, 8),
         ),
         mixing[0], small,
         vmem=8 << 20,
     )
-    block = sent + levels // 2 * LANES // cells
-    up, dn, ext, q0 = call(
+    sides = levels // 2 * LANES // cells
+    block = sent - (ext_rows - sides)
+    up, dn, far, ext, q0, extra = call(
         side_body,
         (
             shape(block, cells),
             shape(block, cells),
+            shape(block + ext_rows, cells),
             shape(ext_rows, cells + LANES),
             shape(8, cells),
+            shape(ext_rows, cells + LANES),
         ),
         xin, from_right, from_left, fields, face0,
         scratch=[pltpu.VMEM((levels, LANES), F32)],
         vmem=8 << 20,
     )
 
-    hop = lax.ppermute(ext, axes, [(at(0, r, s), at(1, r, s)) for r, s in spots])
+    swap = [(at(g, r, s), at(1 - g, r, s)) for g in range(2) for r, s in spots]
+    hop = lax.ppermute(ext, axes, swap)
     line = lax.broadcasted_iota(jnp.int32, ext.shape, 0)
     relay = jnp.where((line >= nf * STEPS) & (line < nf * (STEPS + 1)), ext, hop)
+    relay = jnp.where(lax.axis_index("grp") == 1, relay, extra)
     got, mains = {0: hop}, {}
     for d in sorted(range(-near, near + 1), key=abs):
         key = d % n_reg
         if key in got:
             continue
-        pairs = [(at(1, r + d, s), at(1, r, s)) for r, s in spots]
-        got[key] = lax.ppermute(relay, axes, pairs)
-        groups = (0, 1) if abs(d) == 1 else (0,)
-        pairs = [(at(g, r + d, s), at(g, r, s)) for g in groups for r, s in spots]
-        mains[key] = lax.ppermute(up if d < 0 else dn, axes, pairs)
+        close = abs(d) == 1
+        ring = [[(at(g, r + d, s), at(g, r, s)) for r, s in spots] for g in (0, 1)]
+        both = ring[0] + ring[1]
+        got[key] = lax.ppermute(relay, axes, both if close else ring[1])
+        block_sent = (up if d < 0 else dn) if close else far
+        mains[key] = lax.ppermute(block_sent, axes, both if close else ring[0])
     ext_blocks = [got[d % n_reg] for d in range(-near, near + 1)]
     above, below = mains[-1 % n_reg], mains[1 % n_reg]
 
@@ -768,7 +805,7 @@
 
     ext_o = up8(rows + 2 * HALO)
     near_sum = call(
-        functools.partial(ocean_body, rows, links, sent),
+        functools.partial(ocean_body, rows, links),
         shape(levels, cells),
         xin, cell_in, above, below, up,
         scratch=[
@@ -812,31 +849,28 @@
     )
     back = lax.ppermute(coupled, axes, [(at(1, r, s), at(0, r, s)) for r, s in spots])
 
-    wide = 3 * rows * WIDE
-    ext_i = up8(3 * rows)
-    x0, x1, x2 = call(
+    spread = shape(sent, total * WIDE)
+    taps = shape(TAPS * TAPS, 8 * n, WIDE)
+    basis = shape(packed, cells, dtype=BF16)
+    early = call(
         functools.partial(inner_body, rows, links, sent, levels),
-        (shape(sent, wide), shape(sent, wide), shape(sent, wide)),
-        above, up, below,
+        (spread, spread, spread, taps, basis, basis),
+        above, up, below, got[-1 % n_reg], extra, got[1 % n_reg],
+        scratch=[pltpu.VMEM((links, 8 * n, WIDE), F32)],
+        vmem=20 << 20,
+    )
+    new_state = call(
+        functools.partial(state_body, rows, links, sent, block),
+        (shape(levels, cells), spread, spread, spread, taps, basis, basis),
+        mains[-2 % n_reg], mains[2 % n_reg], *early, powers, xin, near_sum, own_mix, own_flux,
+        lift, table,
         scratch=[
-            pltpu.VMEM((links, ext_i, WIDE), F32),
-            pltpu.VMEM((TAPS * TAPS, ext_i, WIDE), F32),
+            pltpu.VMEM((sent, total * WIDE), F32),
+            pltpu.VMEM((links, 8 * n, WIDE), F32),
         ],
-        vmem=12 << 20,
-    )
-    new_state = call(
-        functools.partial(state_body, rows, links, sent),
-        shape(levels, cells),
-        mains[-2 % n_reg], mains[2 % n_reg], x0, x1, x2, powers, xin, near_sum, own_mix, own_flux,
-        lift, table,
-        scratch=[pltpu.VMEM((sent, total * WIDE), F32) for _ in range(4)]
-        + [
-            pltpu.VMEM((links, ext_n, WIDE), F32),
-            pltpu.VMEM((TAPS * TAPS, ext_n, WIDE), F32),
-            pltpu.VMEM(((STEPS + 1) * levels, cells), F32),
-        ],
+        alias={2 + k: 1 + k for k in range(6)},
         vmem=24 << 20,
-    )
+    )[0]
     ocean_side = lax.axis_index("grp") == 1
     surface = jnp.where(ocean_side, coupled[:nr], back[:nr])
     return (new_state[None], surface)

time: 57.7 us -> 61.7 us (1.069)
  the two profiles are of different devices: /device:TPU:0 before, /device:TPU:9 now
where the time goes in v1:
time: 61.7 us; the launch traced here: 61.3 us
  waiting for transfers between devices  22.8 us (37%)
  starting transfers between devices  17.5 us (28%)
  Pallas kernels  14.5 us (24%)
  local copies, waits for them, and re-layouts  3.39 us (5%)
  other arithmetic  2.22 us (4%)
  between operations  0.77 us (1%)
    pallas_call x10, Pallas kernels, call(): pl.pallas_call(body, out_shape=outs, in_specs=[pl.BlockSpec(memory_space=...  14.5 us
    ppermute x3, waiting for transfers between devices, local(): mains[key] = lax.ppermute(block_sent, axes, both if close else ring[0])  13 us
    ppermute x6, starting transfers between devices, shift(): return lax.ppermute(x, axis, [((i + d) % size, i) for i in range(size)])  7.33 us
    ppermute x3, starting transfers between devices, local(): mains[key] = lax.ppermute(block_sent, axes, both if close else ring[0])  6.1 us
    unnamed x7, local copies, waits for them, and re-layouts  3.32 us
    ppermute x1, waiting for transfers between devices, local(): lax.ppermute(coupled, axes, [(at(1, r, s), at(0, r, s)) for r, s in spots])  3.27 us
    ppermute x3, waiting for transfers between devices, local(): got[key] = lax.ppermute(relay, axes, both if close else ring[1])  3.17 us
    ppermute x1, waiting for transfers between devices, local(): hop = lax.ppermute(ext, axes, swap)  2.48 us
  transfers between devices with their start and end apart: 14, of which 6 were waited for; matrix products, arithmetic and copies ran while one was open for 2% of the time, Pallas kernels for 9%

profile of v1, /device:TPU:9, one launch (start us, length us, event | category | flops | bytes accessed | tf_op | source)
XLA Modules:
  0.0 61.3 jit_solution(5502910399094199476)
XLA Ops:
  0.7 0.7 %copy.20 = s32[1,3,512]{2,1,0:T(4,128)S(1)} copy(s32[1,3,512]{2,0,1:T(1,128)} %param.11) | data formatting | bytes 12288
  1.4 0.8 %pad_add_fusion.cell_in.refs_7_ = f32[16,512]{1,0:T(8,128)S(1)} fusion(f32[3,512]{1,0:T(4,128)} %param.18, s32[1,512]{1,0:T(1,128)} %bitcast.13, s32[3,512]{1,0:T(4,128)} %param.17, s32[3,512]{1,0:T(4,128)S(1)} %bitcast.11, s32[16]{0:T(128)S(1)} %pad.40), kind=kLoop, calls=%fused_computation.1 | loop fusion | flops 40960 | bytes 53312 | tf_op jit(solution)/shard_map/add | solution.py:722
  2.2 0.9 %copy-done = f32[1,128,512]{2,1,0:T(8,128)S(1)} copy-done((f32[1,128,512]{2,1,0:T(8,128)S(1)}, f32[1,128,512]{2,1,0:T(8,128)}, u32[]{:S(2)}) %copy-start) | copy-done | bytes 262168
  3.2 0.2 shard_map.113
  3.4 0.7 %collective-permute-start = (f32[64,128]{1,0:T(8,128)S(1)}, f32[64,128]{1,0:T(8,128)S(1)}, u32[]{:S(2)}, u32[]{:S(2)}) collective-permute-start(f32[64,128]{1,0:T(8,128)S(1)} %get-tuple-element.30), channel_id=1, source_target_pairs={{1,0},{2,1},{3,2},{0,3},{5,4},{6,5},{7,6},{4,7},{9,8},{10,9},{11,1... | collective-permute-start | bytes 98312 | tf_op jit(solution)/shard_map/ppermute | solution.py:709
  4.1 1.2 %collective-permute-start.1 = (f32[64,128]{1,0:T(8,128)S(1)}, f32[64,128]{1,0:T(8,128)S(1)}, u32[]{:S(2)}, u32[]{:S(2)}) collective-permute-start(f32[64,128]{1,0:T(8,128)S(1)} %get-tuple-element.31), channel_id=1, source_target_pairs={{3,0},{0,1},{1,2},{2,3},{7,4},{4,5},{5,6},{6,7},{11,8},{8,9},{9,10... | collective-permute-start | bytes 98312 | tf_op jit(solution)/shard_map/ppermute | solution.py:709
  5.3 0.7 %pad_add_fusion.1.small = f32[16,128]{1,0:T(8,128)S(1)} fusion(f32[3,128]{1,0:T(4,128)} %param.16, f32[4,128]{1,0:T(4,128)} %bitcast.12, f32[4,128]{1,0:T(4,128)} %param.14, f32[1,128]{1,0:T(1,128)} %param.13), kind=kLoop, calls=%fused_computation.4 | loop fusion | flops 6144 | bytes 14336 | tf_op jit(solution)/shard_map/add | solution.py:716
  6.0 0.8 %copy-done.1 = f32[1,128,128]{2,1,0:T(8,128)S(1)} copy-done((f32[1,128,128]{2,1,0:T(8,128)S(1)}, f32[1,128,128]{2,1,0:T(8,128)}, u32[]{:S(2)}) %copy-start.1) | copy-done | bytes 65560
  6.8 0.8 %shard_map.114 = (f32[24,128]{1,0:T(8,128)S(1)}, f32[8,128]{1,0:T(8,128)S(1)}) custom-call(f32[128,128]{1,0:T(8,128)S(1)} %bitcast.9, f32[16,128]{1,0:T(8,128)S(1)} %pad_add_fusion.1.small), custom_call_target="tpu_custom_call" | custom-call | flops 100000 | bytes 73728 | tf_op jit(solution)/shard_map/pallas_call | solution.py:41
  7.7 0.3 shard_map.115
  8.0 0.7 %collective-permute-start.5 = (f32[24,640]{1,0:T(8,128)S(1)}, f32[24,640]{1,0:T(8,128)S(1)}, u32[]{:S(2)}, u32[]{:S(2)}) collective-permute-start(f32[24,640]{1,0:T(8,128)S(1)} %get-tuple-element.37.refs_5_), channel_id=1, source_target_pairs={{0,16},{1,17},{2,18},{3,19},{4,20},{5,21},{6,22},{7,23},{8,24},{9,... | collective-permute-start | bytes 184328 | tf_op jit(solution)/shard_map/ppermute | solution.py:776
  8.7 2.5 %collective-permute-done.5.refs_2_ = f32[24,640]{1,0:T(8,128)S(1)} collective-permute-done((f32[24,640]{1,0:T(8,128)S(1)}, f32[24,640]{1,0:T(8,128)S(1)}, u32[]{:S(2)}, u32[]{:S(2)}) %collective-permute-start.5) | collective-permute-done | bytes 61472 | tf_op jit(solution)/shard_map/ppermute | solution.py:776
  11.2 0.7 %collective-permute-start.8 = (f32[24,640]{1,0:T(8,128)S(1)}, f32[24,640]{1,0:T(8,128)S(1)}, u32[]{:S(2)}, u32[]{:S(2)}) collective-permute-start(f32[24,640]{1,0:T(8,128)S(1)} %select_select_fusion), channel_id=1, source_target_pairs={{24,16},{25,17},{26,18},{27,19},{28,20},{29,21},{30,22},{31,23},{1... | collective-permute-start | bytes 184328 | tf_op jit(solution)/shard_map/ppermute | solution.py:788
  11.9 0.2 collective-permute-start.7
  12.1 1.3 %collective-permute-start.6 = (f32[24,640]{1,0:T(8,128)S(1)}, f32[24,640]{1,0:T(8,128)S(1)}, u32[]{:S(2)}, u32[]{:S(2)}) collective-permute-start(f32[24,640]{1,0:T(8,128)S(1)} %select_select_fusion), channel_id=1, source_target_pairs={{12,0},{13,1},{14,2},{15,3},{0,4},{1,5},{2,6},{3,7},{4,8},{5,9},{6... | collective-permute-start | bytes 184328 | tf_op jit(solution)/shard_map/ppermute | solution.py:788
  13.4 1.1 %collective-permute-start.12 = (f32[8,512]{1,0:T(8,128)S(1)}, f32[8,512]{1,0:T(8,128)S(1)}, u32[]{:S(2)}, u32[]{:S(2)}) collective-permute-start(f32[8,512]{1,0:T(8,128)S(1)} %get-tuple-element.48.refs_0_.table), channel_id=1, source_target_pairs={{2,0},{3,1},{0,2},{1,3},{6,4},{7,5},{4,6},{5,7},{10,8},{11,9},{8,1... | collective-permute-start | bytes 49160 | tf_op jit(solution)/shard_map/ppermute | solution.py:709
  14.5 0.5 collective-permute-done.7.more_below.refs_3_
  15.0 2.7 %collective-permute-done.6.more_above.refs_1_ = f32[24,640]{1,0:T(8,128)S(1)} collective-permute-done((f32[24,640]{1,0:T(8,128)S(1)}, f32[24,640]{1,0:T(8,128)S(1)}, u32[]{:S(2)}, u32[]{:S(2)}) %collective-permute-start.6) | collective-permute-done | bytes 61472 | tf_op jit(solution)/shard_map/ppermute | solution.py:788
  17.7 3.5 %collective-permute-start.11 = (f32[8,512]{1,0:T(8,128)S(1)}, f32[8,512]{1,0:T(8,128)S(1)}, u32[]{:S(2)}, u32[]{:S(2)}) collective-permute-start(f32[8,512]{1,0:T(8,128)S(1)} %shard_map.119.refs_0_), channel_id=1, source_target_pairs={{3,0},{0,1},{1,2},{2,3},{7,4},{4,5},{5,6},{6,7},{11,8},{8,9},{9,10... | collective-permute-start | bytes 49160 | tf_op jit(solution)/shard_map/ppermute | solution.py:709
  21.2 0.8 %collective-permute-start.10 = (f32[8,512]{1,0:T(8,128)S(1)}, f32[8,512]{1,0:T(8,128)S(1)}, u32[]{:S(2)}, u32[]{:S(2)}) collective-permute-start(f32[8,512]{1,0:T(8,128)S(1)} %shard_map.119.refs_0_), channel_id=1, source_target_pairs={{2,0},{3,1},{0,2},{1,3},{6,4},{7,5},{4,6},{5,7},{10,8},{11,9},{8,1... | collective-permute-start | bytes 49160 | tf_op jit(solution)/shard_map/ppermute | solution.py:709
  22.0 0.8 %copy-done.2 = f32[1,128,128]{2,1,0:T(8,128)S(1)} copy-done((f32[1,128,128]{2,1,0:T(8,128)S(1)}, f32[1,128,128]{2,1,0:T(8,128)}, u32[]{:S(2)}) %copy-start.2) | copy-done | bytes 65560
  22.9 1.4 %shard_map.117 = (bf16[192,512]{1,0:T(8,128)(2,1)S(1)}, f32[128,256]{1,0:T(8,128)S(1)}, f32[136,8]{1,0:T(8,128)S(1)}) custom-call(f32[128,128]{1,0:T(8,128)S(1)} %bitcast.10, f32[16,128]{1,0:T(8,128)S(1)} %pad_add_fusion.1.small), custom_call_target="tpu_custom_call" | custom-call | flops 100000 | bytes 73728 | tf_op jit(solution)/shard_map/pallas_call | solution.py:41
  24.3 0.9 %collective-permute-done.9.refs_1_ = f32[8,512]{1,0:T(8,128)S(1)} collective-permute-done((f32[8,512]{1,0:T(8,128)S(1)}, f32[8,512]{1,0:T(8,128)S(1)}, u32[]{:S(2)}, u32[]{:S(2)}) %collective-permute-start.9) | collective-permute-done | bytes 16416 | tf_op jit(solution)/shard_map/ppermute | solution.py:709
  25.2 1.3 %collective-permute-start.13 = (f32[8,512]{1,0:T(8,128)S(1)}, f32[8,512]{1,0:T(8,128)S(1)}, u32[]{:S(2)}, u32[]{:S(2)}) collective-permute-start(f32[8,512]{1,0:T(8,128)S(1)} %get-tuple-element.55), channel_id=1, source_target_pairs={{16,0},{17,1},{18,2},{19,3},{20,4},{21,5},{22,6},{23,7},{24,8},{25... | collective-permute-start | bytes 49160 | tf_op jit(solution)/shard_map/ppermute | solution.py:850
  26.5 3.3 %collective-permute-start.2 = (f32[112,512]{1,0:T(8,128)S(1)}, f32[112,512]{1,0:T(8,128)S(1)}, u32[]{:S(2)}, u32[]{:S(2)}) collective-permute-start(f32[112,512]{1,0:T(8,128)S(1)} %get-tuple-element.34), channel_id=1, source_target_pairs={{8,0},{9,1},{10,2},{11,3},{12,4},{13,5},{14,6},{15,7},{0,8},{1,9},... | collective-permute-start | bytes 688136 | tf_op jit(solution)/shard_map/ppermute | solution.py:790
  29.8 1.5 %collective-permute-start.4 = (f32[88,512]{1,0:T(8,128)S(1)}, f32[88,512]{1,0:T(8,128)S(1)}, u32[]{:S(2)}, u32[]{:S(2)}) collective-permute-start(f32[88,512]{1,0:T(8,128)S(1)} %get-tuple-element.36), channel_id=1, source_target_pairs={{4,0},{5,1},{6,2},{7,3},{8,4},{9,5},{10,6},{11,7},{12,8},{13,9},{1... | collective-permute-start | bytes 540680 | tf_op jit(solution)/shard_map/ppermute | solution.py:790
  31.3 1.2 %collective-permute-start.3 = (f32[88,512]{1,0:T(8,128)S(1)}, f32[88,512]{1,0:T(8,128)S(1)}, u32[]{:S(2)}, u32[]{:S(2)}) collective-permute-start(f32[88,512]{1,0:T(8,128)S(1)} %get-tuple-element.35.own), channel_id=1, source_target_pairs={{12,0},{13,1},{14,2},{15,3},{0,4},{1,5},{2,6},{3,7},{4,8},{5,9},{6... | collective-permute-start | bytes 540680 | tf_op jit(solution)/shard_map/ppermute | solution.py:790
  32.6 3.3 %collective-permute-done.13 = f32[8,512]{1,0:T(8,128)S(1)} collective-permute-done((f32[8,512]{1,0:T(8,128)S(1)}, f32[8,512]{1,0:T(8,128)S(1)}, u32[]{:S(2)}, u32[]{:S(2)}) %collective-permute-start.13) | collective-permute-done | bytes 16416 | tf_op jit(solution)/shard_map/ppermute | solution.py:850
  35.8 0.6 slice_select_fusion
  36.4 13.0 %collective-permute-done.4.below = f32[88,512]{1,0:T(8,128)S(1)} collective-permute-done((f32[88,512]{1,0:T(8,128)S(1)}, f32[88,512]{1,0:T(8,128)S(1)}, u32[]{:S(2)}, u32[]{:S(2)}) %collective-permute-start.4) | collective-permute-done | bytes 180256 | tf_op jit(solution)/shard_map/ppermute | solution.py:790
  49.5 3.6 %shard_map.116 = (f32[96,5120]{1,0:T(8,128)S(1)}, f32[96,5120]{1,0:T(8,128)S(1)}, f32[96,5120]{1,0:T(8,128)S(1)}, f32[25,40,256]{2,1,0:T(8,128)S(1)}, bf16[512,5...) custom-call(f32[88,512]{1,0:T(8,128)S(1)} %collective-permute-done.3.above, f32[88,512]{1,0:T(8,128)S(1)} %get-tuple-element.35.own, ...), custom_call_target="tpu_custom_call" | custom-call | flops 100000 | bytes 724992 | tf_op jit(solution)/shard_map/pallas_call | solution.py:41
  53.0 8.2 %shard_map.122 = (f32[128,512]{1,0:T(8,128)}, f32[96,5120]{1,0:T(8,128)S(1)}, f32[96,5120]{1,0:T(8,128)S(1)}, f32[96,5120]{1,0:T(8,128)S(1)}, f32[25,40,256]{2,1...) custom-call(f32[112,512]{1,0:T(8,128)S(1)} %collective-permute-done., ...), custom_call_target="tpu_custom_call", output_to_operand_aliasing={{1}: (2, {}), {2}: (3, {}), {3}: (4, {}), {4}: (5, {}), {5}... | custom-call | flops 100000 | bytes 9318656 | tf_op jit(solution)/shard_map/pallas_call | solution.py:41
  (20 shorter events, 0.2 us)
Async XLA Ops:
  2.2 0.9 %copy-start = (f32[1,128,512]{2,1,0:T(8,128)S(1)}, f32[1,128,512]{2,1,0:T(8,128)}, u32[]{:S(2)}) copy-start(f32[1,128,512]{2,1,0:T(8,128)} %param.10) | copy-start | bytes 786436
  3.4 4.3 %collective-permute-start = (f32[64,128]{1,0:T(8,128)S(1)}, f32[64,128]{1,0:T(8,128)S(1)}, u32[]{:S(2)}, u32[]{:S(2)}) collective-permute-start(f32[64,128]{1,0:T(8,128)S(1)} %get-tuple-element.30), channel_id=1, source_target_pairs={{1,0},{2,1},{3,2},{0,3},{5,4},{6,5},{7,6},{4,7},{9,8},{10,9},{11,1... | collective-permute-start | bytes 98312 | tf_op jit(solution)/shard_map/ppermute | solution.py:709
  4.1 3.6 %collective-permute-start.1 = (f32[64,128]{1,0:T(8,128)S(1)}, f32[64,128]{1,0:T(8,128)S(1)}, u32[]{:S(2)}, u32[]{:S(2)}) collective-permute-start(f32[64,128]{1,0:T(8,128)S(1)} %get-tuple-element.31), channel_id=1, source_target_pairs={{3,0},{0,1},{1,2},{2,3},{7,4},{4,5},{5,6},{6,7},{11,8},{8,9},{9,10... | collective-permute-start | bytes 98312 | tf_op jit(solution)/shard_map/ppermute | solution.py:709
  6.0 0.8 %copy-start.1 = (f32[1,128,128]{2,1,0:T(8,128)S(1)}, f32[1,128,128]{2,1,0:T(8,128)}, u32[]{:S(2)}) copy-start(f32[1,128,128]{2,1,0:T(8,128)} %param.12) | copy-start | bytes 196612
  8.0 3.1 %collective-permute-start.5 = (f32[24,640]{1,0:T(8,128)S(1)}, f32[24,640]{1,0:T(8,128)S(1)}, u32[]{:S(2)}, u32[]{:S(2)}) collective-permute-start(f32[24,640]{1,0:T(8,128)S(1)} %get-tuple-element.37.refs_5_), channel_id=1, source_target_pairs={{0,16},{1,17},{2,18},{3,19},{4,20},{5,21},{6,22},{7,23},{8,24},{9,... | collective-permute-start | bytes 184328 | tf_op jit(solution)/shard_map/ppermute | solution.py:776
  11.2 3.3 %collective-permute-start.8 = (f32[24,640]{1,0:T(8,128)S(1)}, f32[24,640]{1,0:T(8,128)S(1)}, u32[]{:S(2)}, u32[]{:S(2)}) collective-permute-start(f32[24,640]{1,0:T(8,128)S(1)} %select_select_fusion), channel_id=1, source_target_pairs={{24,16},{25,17},{26,18},{27,19},{28,20},{29,21},{30,22},{31,23},{1... | collective-permute-start | bytes 184328 | tf_op jit(solution)/shard_map/ppermute | solution.py:788
  11.9 3.1 %collective-permute-start.7 = (f32[24,640]{1,0:T(8,128)S(1)}, f32[24,640]{1,0:T(8,128)S(1)}, u32[]{:S(2)}, u32[]{:S(2)}) collective-permute-start(f32[24,640]{1,0:T(8,128)S(1)} %select_select_fusion), channel_id=1, source_target_pairs={{4,0},{5,1},{6,2},{7,3},{8,4},{9,5},{10,6},{11,7},{12,8},{13,9},{1... | collective-permute-start | bytes 184328 | tf_op jit(solution)/shard_map/ppermute | solution.py:788
  12.1 5.6 %collective-permute-start.6 = (f32[24,640]{1,0:T(8,128)S(1)}, f32[24,640]{1,0:T(8,128)S(1)}, u32[]{:S(2)}, u32[]{:S(2)}) collective-permute-start(f32[24,640]{1,0:T(8,128)S(1)} %select_select_fusion), channel_id=1, source_target_pairs={{12,0},{13,1},{14,2},{15,3},{0,4},{1,5},{2,6},{3,7},{4,8},{5,9},{6... | collective-permute-start | bytes 184328 | tf_op jit(solution)/shard_map/ppermute | solution.py:788
  13.4 10.8 %collective-permute-start.12 = (f32[8,512]{1,0:T(8,128)S(1)}, f32[8,512]{1,0:T(8,128)S(1)}, u32[]{:S(2)}, u32[]{:S(2)}) collective-permute-start(f32[8,512]{1,0:T(8,128)S(1)} %get-tuple-element.48.refs_0_.table), channel_id=1, source_target_pairs={{2,0},{3,1},{0,2},{1,3},{6,4},{7,5},{4,6},{5,7},{10,8},{11,9},{8,1... | collective-permute-start | bytes 49160 | tf_op jit(solution)/shard_map/ppermute | solution.py:709
  17.7 6.6 %collective-permute-start.11 = (f32[8,512]{1,0:T(8,128)S(1)}, f32[8,512]{1,0:T(8,128)S(1)}, u32[]{:S(2)}, u32[]{:S(2)}) collective-permute-start(f32[8,512]{1,0:T(8,128)S(1)} %shard_map.119.refs_0_), channel_id=1, source_target_pairs={{3,0},{0,1},{1,2},{2,3},{7,4},{4,5},{5,6},{6,7},{11,8},{8,9},{9,10... | collective-permute-start | bytes 49160 | tf_op jit(solution)/shard_map/ppermute | solution.py:709
  21.2 3.1 %collective-permute-start.10 = (f32[8,512]{1,0:T(8,128)S(1)}, f32[8,512]{1,0:T(8,128)S(1)}, u32[]{:S(2)}, u32[]{:S(2)}) collective-permute-start(f32[8,512]{1,0:T(8,128)S(1)} %shard_map.119.refs_0_), channel_id=1, source_target_pairs={{2,0},{3,1},{0,2},{1,3},{6,4},{7,5},{4,6},{5,7},{10,8},{11,9},{8,1... | collective-permute-start | bytes 49160 | tf_op jit(solution)/shard_map/ppermute | solution.py:709
  22.0 3.2 %collective-permute-start.9 = (f32[8,512]{1,0:T(8,128)S(1)}, f32[8,512]{1,0:T(8,128)S(1)}, u32[]{:S(2)}, u32[]{:S(2)}) collective-permute-start(f32[8,512]{1,0:T(8,128)S(1)} %shard_map.119.refs_0_), channel_id=1, source_target_pairs={{1,0},{2,1},{3,2},{0,3},{5,4},{6,5},{7,6},{4,7},{9,8},{10,9},{11,1... | collective-permute-start | bytes 49160 | tf_op jit(solution)/shard_map/ppermute | solution.py:709
  22.0 0.8 %copy-start.2 = (f32[1,128,128]{2,1,0:T(8,128)S(1)}, f32[1,128,128]{2,1,0:T(8,128)}, u32[]{:S(2)}) copy-start(f32[1,128,128]{2,1,0:T(8,128)} %param.12) | copy-start | bytes 196612
  25.2 10.7 %collective-permute-start.13 = (f32[8,512]{1,0:T(8,128)S(1)}, f32[8,512]{1,0:T(8,128)S(1)}, u32[]{:S(2)}, u32[]{:S(2)}) collective-permute-start(f32[8,512]{1,0:T(8,128)S(1)} %get-tuple-element.55), channel_id=1, source_target_pairs={{16,0},{17,1},{18,2},{19,3},{20,4},{21,5},{22,6},{23,7},{24,8},{25... | collective-permute-start | bytes 49160 | tf_op jit(solution)/shard_map/ppermute | solution.py:850
  26.5 26.6 %collective-permute-start.2 = (f32[112,512]{1,0:T(8,128)S(1)}, f32[112,512]{1,0:T(8,128)S(1)}, u32[]{:S(2)}, u32[]{:S(2)}) collective-permute-start(f32[112,512]{1,0:T(8,128)S(1)} %get-tuple-element.34), channel_id=1, source_target_pairs={{8,0},{9,1},{10,2},{11,3},{12,4},{13,5},{14,6},{15,7},{0,8},{1,9},... | collective-permute-start | bytes 688136 | tf_op jit(solution)/shard_map/ppermute | solution.py:790
  29.8 19.6 %collective-permute-start.4 = (f32[88,512]{1,0:T(8,128)S(1)}, f32[88,512]{1,0:T(8,128)S(1)}, u32[]{:S(2)}, u32[]{:S(2)}) collective-permute-start(f32[88,512]{1,0:T(8,128)S(1)} %get-tuple-element.36), channel_id=1, source_target_pairs={{4,0},{5,1},{6,2},{7,3},{8,4},{9,5},{10,6},{11,7},{12,8},{13,9},{1... | collective-permute-start | bytes 540680 | tf_op jit(solution)/shard_map/ppermute | solution.py:790
  31.3 18.1 %collective-permute-start.3 = (f32[88,512]{1,0:T(8,128)S(1)}, f32[88,512]{1,0:T(8,128)S(1)}, u32[]{:S(2)}, u32[]{:S(2)}) collective-permute-start(f32[88,512]{1,0:T(8,128)S(1)} %get-tuple-element.35.own), channel_id=1, source_target_pairs={{12,0},{13,1},{14,2},{15,3},{0,4},{1,5},{2,6},{3,7},{4,8},{5,9},{6... | collective-permute-start | bytes 540680 | tf_op jit(solution)/shard_map/ppermute | solution.py:790

commit v2 on v1

--- a/solution.py
+++ b/solution.py
@@ -17,6 +17,7 @@
 BF16 = jnp.bfloat16
 LANES = 128
 WIDE = 2 * LANES
+PACK = LANES // 4
 
 
 def up8(n):
@@ -271,7 +272,7 @@
         )
 
 
-def tap_counts(codes, coef, rows, first_row, links, at=0, count=None):
+def tap_counts(codes, coef, rows, first_row, links, at=0, count=None, packed=False):
     count, wide = count or codes.shape[1], codes.shape[2]
     row = (lax.broadcasted_iota(jnp.int32, (count, wide), 0) + first_row) % rows
     pcol = lax.broadcasted_iota(jnp.int32, (count, wide), 1) % LANES
@@ -287,6 +288,19 @@
             for k in range(links):
                 hits = hits + jnp.where(kinds[k] == dr * 16 + dc, 1.0, 0.0)
             coef[dr * TAPS + dc, at : at + count, :] = roll(hits, dc - HALO)
+    if packed:
+        lane = lane_of(LANES, 8)
+        halo = (lane < RIM) | (lane >= LANES - RIM)
+
+        def pack(o, _):
+            for p in range(TAPS):
+                for a in range(at, at + count, 8):
+                    side = jnp.where(halo, coef[o * TAPS + p, a : a + 8, LANES:], 0.0)
+                    moved = [roll(side, PACK * q) for q in range(1, 4)]
+                    coef[o * TAPS + p, a : a + 8, LANES:] = (side + moved[0]) + (moved[1] + moved[2])
+            return 0
+
+        lax.fori_loop(0, TAPS, pack, 0)
 
 
 def same(i):
@@ -320,6 +334,53 @@
         return 0
 
     lax.fori_loop(0, count // step, one, 0)
+
+
+def stencil_packed(src, dst, coef, groups, first, count, slot):
+    lane = lane_of()
+    edge = (lane < HALO) | (lane >= LANES - HALO)
+
+    def row(i):
+        off = [pl.multiple_of((i + dr - HALO) * WIDE, WIDE) for dr in range(TAPS)]
+        here = pl.multiple_of(i * WIDE, WIDE)
+        for quad in range(groups // 4):
+            acc = {}
+            side = slice(8 * quad, 8 * quad + 8)
+            mains = [slice(8 * g, 8 * g + 8) for g in range(4 * quad, 4 * quad + 4)]
+            for dr in range(TAPS):
+                v = [src[m, pl.ds(off[dr], LANES)] for m in mains]
+                v.append(src[side, pl.ds(off[dr] + LANES, LANES)])
+                for dc in range(TAPS):
+                    c = coef[dr * TAPS + dc, pl.ds(slot(i), 1), :]
+                    for q in range(5):
+                        t = (c[:, 0:LANES] if q < 4 else c[:, LANES:]) * v[q]
+                        acc[q, dc] = t if dr == 0 else acc[q, dc] + t
+            total = [acc[q, HALO] for q in range(5)]
+            crossed = [None] * 5
+            for dc in range(TAPS):
+                d = dc - HALO
+                if d == 0:
+                    continue
+                for q in range(5):
+                    size = LANES if q < 4 else PACK
+                    place = lane if q < 4 else lane % PACK
+                    over = place >= size - d if d > 0 else place < -d
+                    t = roll(acc[q, dc], -d)
+                    total[q] = total[q] + jnp.where(over, 0.0, t)
+                    t = jnp.where(over, t, 0.0)
+                    crossed[q] = t if crossed[q] is None else crossed[q] + t
+            for q in range(4):
+                into = roll(crossed[4], -PACK * q)
+                dst[mains[q], pl.ds(here, LANES)] = total[q] + jnp.where(edge, into, 0.0)
+                total[4] = total[4] + roll(crossed[q], PACK * q)
+            dst[side, pl.ds(here + LANES, LANES)] = total[4]
+
+    def two(o, _):
+        row(first + 2 * o)
+        row(first + 2 * o + 1)
+        return 0
+
+    lax.fori_loop(0, count // 2, two, 0)
 
 
 def chain(xa, xb, coef, groups, rows, near, batch, take, step=1):
@@ -569,24 +630,37 @@
 
 def place_block(x, codes, block, extra, keep, base, b, sent, half, links):
     rows = block.shape[1] // BS
+    span = rows * RIM
+    first = base + half * LANES // block.shape[1] - keep
+    lane = lane_of()
     for i in range(rows):
-        parts = []
+        at = b * rows + i
+        here = slice(i * BS, (i + 1) * BS)
+        total = None
         for g in range(sent // 8):
             part, gs = divmod(8 * g, half)
-            s, lanes = side_spot(0, half, block.shape[1], gs)
-            here = slice(i * BS, (i + 1) * BS)
-            over = 8 * g - keep
-            if over < 0:
+            s, lanes = side_spot(base, half, block.shape[1], gs)
+            if 8 * g < keep:
                 main = block[8 * g : 8 * g + 8, here]
             else:
-                over += base + half * LANES // block.shape[1]
-                main = extra[over : over + 8, here]
-            parts.append((main, extra[base + s : base + s + 8, lanes], part * 2 * rows * RIM))
-        at = b * rows + i
-        place_row(x, i, at, parts, rows)
-        for k in range(links):
-            s = LA + k
-            codes[k, 8 * b + i : 8 * b + i + 1, :] = x[s : s + 1, at * WIDE : (at + 1) * WIDE]
+                main = extra[first + 8 * g : first + 8 * g + 8, here]
+            shift = 2 * span * part + i * RIM
+            x[8 * g : 8 * g + 8, at * WIDE : at * WIDE + LANES] = main
+            if g == LA // 8:
+                side = side_lanes(extra[s : s + 8, lanes], shift, shift + span)
+                for k in range(links):
+                    n = LA % 8 + k
+                    codes[k, 8 * b + i : 8 * b + i + 1, 0:LANES] = main[n : n + 1, :]
+                    codes[k, 8 * b + i : 8 * b + i + 1, LANES:WIDE] = side[n : n + 1, :]
+            if g % 4 == 0:
+                total = jnp.zeros((8, LANES), F32)
+            to = PACK * (g % 4)
+            place = (lane - to) & (LANES - 1)
+            source = extra[s : s + 8, lanes]
+            total = jnp.where(place < RIM, roll(source, to - shift), total)
+            total = jnp.where(place >= LANES - RIM, roll(source, to - RIM - shift - span), total)
+            if g % 4 == 3:
+                x[8 * (g // 4) : 8 * (g // 4) + 8, at * WIDE + LANES : (at + 1) * WIDE] = total
 
 
 def slot_of(rows):
@@ -614,9 +688,9 @@
             place_block(
                 x0, codes, block, extra, block.shape[0], 0, b, sent, levels // 2, links
             )
-        tap_counts(codes, coef, 8, 0, links, 8, 24)
-        stencil(x0, x1, coef, groups, lo + HALO, hi - lo - 2 * HALO, 3, 1, slot)
-        stencil(x1, x2, coef, groups, lo + 2 * HALO, hi - lo - 4 * HALO, 3, 1, slot)
+        tap_counts(codes, coef, 8, 0, links, 8, 24, True)
+        stencil_packed(x0, x1, coef, groups, lo + HALO, hi - lo - 2 * HALO, slot)
+        stencil_packed(x1, x2, coef, groups, lo + 2 * HALO, hi - lo - 4 * HALO, slot)
         used = (STEPS + 1) * sent
         high[used:, :] = jnp.zeros((high.shape[0] - used, high.shape[1]), BF16)
         low[used:, :] = jnp.zeros((high.shape[0] - used, high.shape[1]), BF16)
@@ -648,15 +722,15 @@
         codes[...] = jnp.zeros(codes.shape, F32)
         for b, block in ((0, far_up), (4, far_dn)):
             place_block(x0, codes, block, block, keep, keep, b, sent, levels // 2, links)
-            tap_counts(codes, coef, 8, 0, links, 8 * b, 8)
+            tap_counts(codes, coef, 8, 0, links, 8 * b, 8, True)
 
         def apply(src, dst, j, done=None):
             lo, hi = HALO * j, total - HALO * j
             if done is None:
-                stencil(src, dst, coef, groups, lo, hi - lo, 3, 1, slot)
+                stencil_packed(src, dst, coef, groups, lo, hi - lo, slot)
                 return
-            stencil(src, dst, coef, groups, lo, done[0] - lo, 3, 1, slot)
-            stencil(src, dst, coef, groups, done[1], hi - done[1], 3, 1, slot)
+            stencil_packed(src, dst, coef, groups, lo, done[0] - lo, slot)
+            stencil_packed(src, dst, coef, groups, done[1], hi - done[1], slot)
 
         mid = 2 * rows
         apply(x0, x1, 1, (rows + HALO, 4 * rows - HALO))

time: 61.7 us -> 61.2 us (level)
  transfers between devices with their start and end apart: 14 -> 14, of which waited for: 6 -> 6; matrix products, arithmetic and copies ran while one was open for 2% -> 2% of each run, Pallas kernels for 9% -> 10%
where the time goes in v2:
time: 61.2 us; the launch traced here: 60.8 us
  waiting for transfers between devices  22.8 us (37%)
  starting transfers between devices  17.5 us (29%)
  Pallas kernels  14 us (23%)
  local copies, waits for them, and re-layouts  3.39 us (6%)
  other arithmetic  2.22 us (4%)
  between operations  0.77 us (1%)
    pallas_call x10, Pallas kernels, call(): pl.pallas_call(body, out_shape=outs, in_specs=[pl.BlockSpec(memory_space=...  14 us
    ppermute x3, waiting for transfers between devices, local(): mains[key] = lax.ppermute(block_sent, axes, both if close else ring[0])  13 us
    ppermute x6, starting transfers between devices, shift(): return lax.ppermute(x, axis, [((i + d) % size, i) for i in range(size)])  7.33 us
    ppermute x3, starting transfers between devices, local(): mains[key] = lax.ppermute(block_sent, axes, both if close else ring[0])  6.1 us
    unnamed x7, local copies, waits for them, and re-layouts  3.32 us
    ppermute x1, waiting for transfers between devices, local(): lax.ppermute(coupled, axes, [(at(1, r, s), at(0, r, s)) for r, s in spots])  3.27 us
    ppermute x3, waiting for transfers between devices, local(): got[key] = lax.ppermute(relay, axes, both if close else ring[1])  3.17 us
    ppermute x1, waiting for transfers between devices, local(): hop = lax.ppermute(ext, axes, swap)  2.48 us
  transfers between devices with their start and end apart: 14, of which 6 were waited for; matrix products, arithmetic and copies ran while one was open for 2% of the time, Pallas kernels for 10%

profile of v2, /device:TPU:9, one launch (start us, length us, event | category | flops | bytes accessed | tf_op | source)
XLA Modules:
  0.0 60.8 jit_solution(7141912937885466583)
XLA Ops:
  0.7 0.7 %copy.20 = s32[1,3,512]{2,1,0:T(4,128)S(1)} copy(s32[1,3,512]{2,0,1:T(1,128)} %param.11) | data formatting | bytes 12288
  1.4 0.8 %pad_add_fusion.cell_in.refs_7_ = f32[16,512]{1,0:T(8,128)S(1)} fusion(f32[3,512]{1,0:T(4,128)} %param.18, s32[1,512]{1,0:T(1,128)} %bitcast.13, s32[3,512]{1,0:T(4,128)} %param.17, s32[3,512]{1,0:T(4,128)S(1)} %bitcast.11, s32[16]{0:T(128)S(1)} %pad.40), kind=kLoop, calls=%fused_computation.1 | loop fusion | flops 40960 | bytes 53312 | tf_op jit(solution)/shard_map/add | solution.py:796
  2.2 0.9 %copy-done = f32[1,128,512]{2,1,0:T(8,128)S(1)} copy-done((f32[1,128,512]{2,1,0:T(8,128)S(1)}, f32[1,128,512]{2,1,0:T(8,128)}, u32[]{:S(2)}) %copy-start) | copy-done | bytes 262168
  3.2 0.2 shard_map.113
  3.4 0.7 %collective-permute-start = (f32[64,128]{1,0:T(8,128)S(1)}, f32[64,128]{1,0:T(8,128)S(1)}, u32[]{:S(2)}, u32[]{:S(2)}) collective-permute-start(f32[64,128]{1,0:T(8,128)S(1)} %get-tuple-element.30), channel_id=1, source_target_pairs={{1,0},{2,1},{3,2},{0,3},{5,4},{6,5},{7,6},{4,7},{9,8},{10,9},{11,1... | collective-permute-start | bytes 98312 | tf_op jit(solution)/shard_map/ppermute | solution.py:783
  4.1 1.2 %collective-permute-start.1 = (f32[64,128]{1,0:T(8,128)S(1)}, f32[64,128]{1,0:T(8,128)S(1)}, u32[]{:S(2)}, u32[]{:S(2)}) collective-permute-start(f32[64,128]{1,0:T(8,128)S(1)} %get-tuple-element.31), channel_id=1, source_target_pairs={{3,0},{0,1},{1,2},{2,3},{7,4},{4,5},{5,6},{6,7},{11,8},{8,9},{9,10... | collective-permute-start | bytes 98312 | tf_op jit(solution)/shard_map/ppermute | solution.py:783
  5.3 0.7 %pad_add_fusion.1.small = f32[16,128]{1,0:T(8,128)S(1)} fusion(f32[3,128]{1,0:T(4,128)} %param.16, f32[4,128]{1,0:T(4,128)} %bitcast.12, f32[4,128]{1,0:T(4,128)} %param.14, f32[1,128]{1,0:T(1,128)} %param.13), kind=kLoop, calls=%fused_computation.4 | loop fusion | flops 6144 | bytes 14336 | tf_op jit(solution)/shard_map/add | solution.py:790
  6.0 0.8 %copy-done.1 = f32[1,128,128]{2,1,0:T(8,128)S(1)} copy-done((f32[1,128,128]{2,1,0:T(8,128)S(1)}, f32[1,128,128]{2,1,0:T(8,128)}, u32[]{:S(2)}) %copy-start.1) | copy-done | bytes 65560
  6.8 0.8 %shard_map.114 = (f32[24,128]{1,0:T(8,128)S(1)}, f32[8,128]{1,0:T(8,128)S(1)}) custom-call(f32[128,128]{1,0:T(8,128)S(1)} %bitcast.9, f32[16,128]{1,0:T(8,128)S(1)} %pad_add_fusion.1.small), custom_call_target="tpu_custom_call" | custom-call | flops 100000 | bytes 73728 | tf_op jit(solution)/shard_map/pallas_call | solution.py:42
  7.7 0.3 shard_map.115
  8.0 0.7 %collective-permute-start.5 = (f32[24,640]{1,0:T(8,128)S(1)}, f32[24,640]{1,0:T(8,128)S(1)}, u32[]{:S(2)}, u32[]{:S(2)}) collective-permute-start(f32[24,640]{1,0:T(8,128)S(1)} %get-tuple-element.37.refs_5_), channel_id=1, source_target_pairs={{0,16},{1,17},{2,18},{3,19},{4,20},{5,21},{6,22},{7,23},{8,24},{9,... | collective-permute-start | bytes 184328 | tf_op jit(solution)/shard_map/ppermute | solution.py:850
  8.7 2.5 %collective-permute-done.5.refs_2_ = f32[24,640]{1,0:T(8,128)S(1)} collective-permute-done((f32[24,640]{1,0:T(8,128)S(1)}, f32[24,640]{1,0:T(8,128)S(1)}, u32[]{:S(2)}, u32[]{:S(2)}) %collective-permute-start.5) | collective-permute-done | bytes 61472 | tf_op jit(solution)/shard_map/ppermute | solution.py:850
  11.2 0.7 %collective-permute-start.8 = (f32[24,640]{1,0:T(8,128)S(1)}, f32[24,640]{1,0:T(8,128)S(1)}, u32[]{:S(2)}, u32[]{:S(2)}) collective-permute-start(f32[24,640]{1,0:T(8,128)S(1)} %select_select_fusion), channel_id=1, source_target_pairs={{24,16},{25,17},{26,18},{27,19},{28,20},{29,21},{30,22},{31,23},{1... | collective-permute-start | bytes 184328 | tf_op jit(solution)/shard_map/ppermute | solution.py:862
  11.9 0.2 collective-permute-start.7
  12.1 1.3 %collective-permute-start.6 = (f32[24,640]{1,0:T(8,128)S(1)}, f32[24,640]{1,0:T(8,128)S(1)}, u32[]{:S(2)}, u32[]{:S(2)}) collective-permute-start(f32[24,640]{1,0:T(8,128)S(1)} %select_select_fusion), channel_id=1, source_target_pairs={{12,0},{13,1},{14,2},{15,3},{0,4},{1,5},{2,6},{3,7},{4,8},{5,9},{6... | collective-permute-start | bytes 184328 | tf_op jit(solution)/shard_map/ppermute | solution.py:862
  13.4 1.1 %collective-permute-start.12 = (f32[8,512]{1,0:T(8,128)S(1)}, f32[8,512]{1,0:T(8,128)S(1)}, u32[]{:S(2)}, u32[]{:S(2)}) collective-permute-start(f32[8,512]{1,0:T(8,128)S(1)} %get-tuple-element.48.refs_0_.table), channel_id=1, source_target_pairs={{2,0},{3,1},{0,2},{1,3},{6,4},{7,5},{4,6},{5,7},{10,8},{11,9},{8,1... | collective-permute-start | bytes 49160 | tf_op jit(solution)/shard_map/ppermute | solution.py:783
  14.5 0.5 collective-permute-done.7.more_below.refs_3_
  15.0 2.7 %collective-permute-done.6.more_above.refs_1_ = f32[24,640]{1,0:T(8,128)S(1)} collective-permute-done((f32[24,640]{1,0:T(8,128)S(1)}, f32[24,640]{1,0:T(8,128)S(1)}, u32[]{:S(2)}, u32[]{:S(2)}) %collective-permute-start.6) | collective-permute-done | bytes 61472 | tf_op jit(solution)/shard_map/ppermute | solution.py:862
  17.7 3.5 %collective-permute-start.11 = (f32[8,512]{1,0:T(8,128)S(1)}, f32[8,512]{1,0:T(8,128)S(1)}, u32[]{:S(2)}, u32[]{:S(2)}) collective-permute-start(f32[8,512]{1,0:T(8,128)S(1)} %shard_map.119.refs_0_), channel_id=1, source_target_pairs={{3,0},{0,1},{1,2},{2,3},{7,4},{4,5},{5,6},{6,7},{11,8},{8,9},{9,10... | collective-permute-start | bytes 49160 | tf_op jit(solution)/shard_map/ppermute | solution.py:783
  21.2 0.8 %collective-permute-start.10 = (f32[8,512]{1,0:T(8,128)S(1)}, f32[8,512]{1,0:T(8,128)S(1)}, u32[]{:S(2)}, u32[]{:S(2)}) collective-permute-start(f32[8,512]{1,0:T(8,128)S(1)} %shard_map.119.refs_0_), channel_id=1, source_target_pairs={{2,0},{3,1},{0,2},{1,3},{6,4},{7,5},{4,6},{5,7},{10,8},{11,9},{8,1... | collective-permute-start | bytes 49160 | tf_op jit(solution)/shard_map/ppermute | solution.py:783
  22.0 0.8 %copy-done.2 = f32[1,128,128]{2,1,0:T(8,128)S(1)} copy-done((f32[1,128,128]{2,1,0:T(8,128)S(1)}, f32[1,128,128]{2,1,0:T(8,128)}, u32[]{:S(2)}) %copy-start.2) | copy-done | bytes 65560
  22.9 1.4 %shard_map.117 = (bf16[192,512]{1,0:T(8,128)(2,1)S(1)}, f32[128,256]{1,0:T(8,128)S(1)}, f32[136,8]{1,0:T(8,128)S(1)}) custom-call(f32[128,128]{1,0:T(8,128)S(1)} %bitcast.10, f32[16,128]{1,0:T(8,128)S(1)} %pad_add_fusion.1.small), custom_call_target="tpu_custom_call" | custom-call | flops 100000 | bytes 73728 | tf_op jit(solution)/shard_map/pallas_call | solution.py:42
  24.3 0.9 %collective-permute-done.9.refs_1_ = f32[8,512]{1,0:T(8,128)S(1)} collective-permute-done((f32[8,512]{1,0:T(8,128)S(1)}, f32[8,512]{1,0:T(8,128)S(1)}, u32[]{:S(2)}, u32[]{:S(2)}) %collective-permute-start.9) | collective-permute-done | bytes 16416 | tf_op jit(solution)/shard_map/ppermute | solution.py:783
  25.2 1.3 %collective-permute-start.13 = (f32[8,512]{1,0:T(8,128)S(1)}, f32[8,512]{1,0:T(8,128)S(1)}, u32[]{:S(2)}, u32[]{:S(2)}) collective-permute-start(f32[8,512]{1,0:T(8,128)S(1)} %get-tuple-element.55), channel_id=1, source_target_pairs={{16,0},{17,1},{18,2},{19,3},{20,4},{21,5},{22,6},{23,7},{24,8},{25... | collective-permute-start | bytes 49160 | tf_op jit(solution)/shard_map/ppermute | solution.py:924
  26.5 3.3 %collective-permute-start.2 = (f32[112,512]{1,0:T(8,128)S(1)}, f32[112,512]{1,0:T(8,128)S(1)}, u32[]{:S(2)}, u32[]{:S(2)}) collective-permute-start(f32[112,512]{1,0:T(8,128)S(1)} %get-tuple-element.34), channel_id=1, source_target_pairs={{8,0},{9,1},{10,2},{11,3},{12,4},{13,5},{14,6},{15,7},{0,8},{1,9},... | collective-permute-start | bytes 688136 | tf_op jit(solution)/shard_map/ppermute | solution.py:864
  29.8 1.5 %collective-permute-start.4 = (f32[88,512]{1,0:T(8,128)S(1)}, f32[88,512]{1,0:T(8,128)S(1)}, u32[]{:S(2)}, u32[]{:S(2)}) collective-permute-start(f32[88,512]{1,0:T(8,128)S(1)} %get-tuple-element.36), channel_id=1, source_target_pairs={{4,0},{5,1},{6,2},{7,3},{8,4},{9,5},{10,6},{11,7},{12,8},{13,9},{1... | collective-permute-start | bytes 540680 | tf_op jit(solution)/shard_map/ppermute | solution.py:864
  31.3 1.2 %collective-permute-start.3 = (f32[88,512]{1,0:T(8,128)S(1)}, f32[88,512]{1,0:T(8,128)S(1)}, u32[]{:S(2)}, u32[]{:S(2)}) collective-permute-start(f32[88,512]{1,0:T(8,128)S(1)} %get-tuple-element.35.own), channel_id=1, source_target_pairs={{12,0},{13,1},{14,2},{15,3},{0,4},{1,5},{2,6},{3,7},{4,8},{5,9},{6... | collective-permute-start | bytes 540680 | tf_op jit(solution)/shard_map/ppermute | solution.py:864
  32.6 3.3 %collective-permute-done.13 = f32[8,512]{1,0:T(8,128)S(1)} collective-permute-done((f32[8,512]{1,0:T(8,128)S(1)}, f32[8,512]{1,0:T(8,128)S(1)}, u32[]{:S(2)}, u32[]{:S(2)}) %collective-permute-start.13) | collective-permute-done | bytes 16416 | tf_op jit(solution)/shard_map/ppermute | solution.py:924
  35.8 0.6 slice_select_fusion
  36.4 13.0 %collective-permute-done.4.below = f32[88,512]{1,0:T(8,128)S(1)} collective-permute-done((f32[88,512]{1,0:T(8,128)S(1)}, f32[88,512]{1,0:T(8,128)S(1)}, u32[]{:S(2)}, u32[]{:S(2)}) %collective-permute-start.4) | collective-permute-done | bytes 180256 | tf_op jit(solution)/shard_map/ppermute | solution.py:864
  49.5 3.6 %shard_map.116 = (f32[96,5120]{1,0:T(8,128)S(1)}, f32[96,5120]{1,0:T(8,128)S(1)}, f32[96,5120]{1,0:T(8,128)S(1)}, f32[25,40,256]{2,1,0:T(8,128)S(1)}, bf16[512,5...) custom-call(f32[88,512]{1,0:T(8,128)S(1)} %collective-permute-done.3.above, f32[88,512]{1,0:T(8,128)S(1)} %get-tuple-element.35.own, ...), custom_call_target="tpu_custom_call" | custom-call | flops 100000 | bytes 724992 | tf_op jit(solution)/shard_map/pallas_call | solution.py:42
  53.0 7.7 %shard_map.122 = (f32[128,512]{1,0:T(8,128)}, f32[96,5120]{1,0:T(8,128)S(1)}, f32[96,5120]{1,0:T(8,128)S(1)}, f32[96,5120]{1,0:T(8,128)S(1)}, f32[25,40,256]{2,1...) custom-call(f32[112,512]{1,0:T(8,128)S(1)} %collective-permute-done., ...), custom_call_target="tpu_custom_call", output_to_operand_aliasing={{1}: (2, {}), {2}: (3, {}), {3}: (4, {}), {4}: (5, {}), {5}... | custom-call | flops 100000 | bytes 9318656 | tf_op jit(solution)/shard_map/pallas_call | solution.py:42
  (20 shorter events, 0.2 us)
Async XLA Ops:
  2.2 0.9 %copy-start = (f32[1,128,512]{2,1,0:T(8,128)S(1)}, f32[1,128,512]{2,1,0:T(8,128)}, u32[]{:S(2)}) copy-start(f32[1,128,512]{2,1,0:T(8,128)} %param.10) | copy-start | bytes 786436
  3.4 4.3 %collective-permute-start = (f32[64,128]{1,0:T(8,128)S(1)}, f32[64,128]{1,0:T(8,128)S(1)}, u32[]{:S(2)}, u32[]{:S(2)}) collective-permute-start(f32[64,128]{1,0:T(8,128)S(1)} %get-tuple-element.30), channel_id=1, source_target_pairs={{1,0},{2,1},{3,2},{0,3},{5,4},{6,5},{7,6},{4,7},{9,8},{10,9},{11,1... | collective-permute-start | bytes 98312 | tf_op jit(solution)/shard_map/ppermute | solution.py:783
  4.1 3.6 %collective-permute-start.1 = (f32[64,128]{1,0:T(8,128)S(1)}, f32[64,128]{1,0:T(8,128)S(1)}, u32[]{:S(2)}, u32[]{:S(2)}) collective-permute-start(f32[64,128]{1,0:T(8,128)S(1)} %get-tuple-element.31), channel_id=1, source_target_pairs={{3,0},{0,1},{1,2},{2,3},{7,4},{4,5},{5,6},{6,7},{11,8},{8,9},{9,10... | collective-permute-start | bytes 98312 | tf_op jit(solution)/shard_map/ppermute | solution.py:783
  6.0 0.8 %copy-start.1 = (f32[1,128,128]{2,1,0:T(8,128)S(1)}, f32[1,128,128]{2,1,0:T(8,128)}, u32[]{:S(2)}) copy-start(f32[1,128,128]{2,1,0:T(8,128)} %param.12) | copy-start | bytes 196612
  8.0 3.1 %collective-permute-start.5 = (f32[24,640]{1,0:T(8,128)S(1)}, f32[24,640]{1,0:T(8,128)S(1)}, u32[]{:S(2)}, u32[]{:S(2)}) collective-permute-start(f32[24,640]{1,0:T(8,128)S(1)} %get-tuple-element.37.refs_5_), channel_id=1, source_target_pairs={{0,16},{1,17},{2,18},{3,19},{4,20},{5,21},{6,22},{7,23},{8,24},{9,... | collective-permute-start | bytes 184328 | tf_op jit(solution)/shard_map/ppermute | solution.py:850
  11.2 3.3 %collective-permute-start.8 = (f32[24,640]{1,0:T(8,128)S(1)}, f32[24,640]{1,0:T(8,128)S(1)}, u32[]{:S(2)}, u32[]{:S(2)}) collective-permute-start(f32[24,640]{1,0:T(8,128)S(1)} %select_select_fusion), channel_id=1, source_target_pairs={{24,16},{25,17},{26,18},{27,19},{28,20},{29,21},{30,22},{31,23},{1... | collective-permute-start | bytes 184328 | tf_op jit(solution)/shard_map/ppermute | solution.py:862
  11.9 3.1 %collective-permute-start.7 = (f32[24,640]{1,0:T(8,128)S(1)}, f32[24,640]{1,0:T(8,128)S(1)}, u32[]{:S(2)}, u32[]{:S(2)}) collective-permute-start(f32[24,640]{1,0:T(8,128)S(1)} %select_select_fusion), channel_id=1, source_target_pairs={{4,0},{5,1},{6,2},{7,3},{8,4},{9,5},{10,6},{11,7},{12,8},{13,9},{1... | collective-permute-start | bytes 184328 | tf_op jit(solution)/shard_map/ppermute | solution.py:862
  12.1 5.6 %collective-permute-start.6 = (f32[24,640]{1,0:T(8,128)S(1)}, f32[24,640]{1,0:T(8,128)S(1)}, u32[]{:S(2)}, u32[]{:S(2)}) collective-permute-start(f32[24,640]{1,0:T(8,128)S(1)} %select_select_fusion), channel_id=1, source_target_pairs={{12,0},{13,1},{14,2},{15,3},{0,4},{1,5},{2,6},{3,7},{4,8},{5,9},{6... | collective-permute-start | bytes 184328 | tf_op jit(solution)/shard_map/ppermute | solution.py:862
  13.4 10.8 %collective-permute-start.12 = (f32[8,512]{1,0:T(8,128)S(1)}, f32[8,512]{1,0:T(8,128)S(1)}, u32[]{:S(2)}, u32[]{:S(2)}) collective-permute-start(f32[8,512]{1,0:T(8,128)S(1)} %get-tuple-element.48.refs_0_.table), channel_id=1, source_target_pairs={{2,0},{3,1},{0,2},{1,3},{6,4},{7,5},{4,6},{5,7},{10,8},{11,9},{8,1... | collective-permute-start | bytes 49160 | tf_op jit(solution)/shard_map/ppermute | solution.py:783
  17.7 6.6 %collective-permute-start.11 = (f32[8,512]{1,0:T(8,128)S(1)}, f32[8,512]{1,0:T(8,128)S(1)}, u32[]{:S(2)}, u32[]{:S(2)}) collective-permute-start(f32[8,512]{1,0:T(8,128)S(1)} %shard_map.119.refs_0_), channel_id=1, source_target_pairs={{3,0},{0,1},{1,2},{2,3},{7,4},{4,5},{5,6},{6,7},{11,8},{8,9},{9,10... | collective-permute-start | bytes 49160 | tf_op jit(solution)/shard_map/ppermute | solution.py:783
  21.2 3.1 %collective-permute-start.10 = (f32[8,512]{1,0:T(8,128)S(1)}, f32[8,512]{1,0:T(8,128)S(1)}, u32[]{:S(2)}, u32[]{:S(2)}) collective-permute-start(f32[8,512]{1,0:T(8,128)S(1)} %shard_map.119.refs_0_), channel_id=1, source_target_pairs={{2,0},{3,1},{0,2},{1,3},{6,4},{7,5},{4,6},{5,7},{10,8},{11,9},{8,1... | collective-permute-start | bytes 49160 | tf_op jit(solution)/shard_map/ppermute | solution.py:783
  22.0 3.2 %collective-permute-start.9 = (f32[8,512]{1,0:T(8,128)S(1)}, f32[8,512]{1,0:T(8,128)S(1)}, u32[]{:S(2)}, u32[]{:S(2)}) collective-permute-start(f32[8,512]{1,0:T(8,128)S(1)} %shard_map.119.refs_0_), channel_id=1, source_target_pairs={{1,0},{2,1},{3,2},{0,3},{5,4},{6,5},{7,6},{4,7},{9,8},{10,9},{11,1... | collective-permute-start | bytes 49160 | tf_op jit(solution)/shard_map/ppermute | solution.py:783
  22.0 0.8 %copy-start.2 = (f32[1,128,128]{2,1,0:T(8,128)S(1)}, f32[1,128,128]{2,1,0:T(8,128)}, u32[]{:S(2)}) copy-start(f32[1,128,128]{2,1,0:T(8,128)} %param.12) | copy-start | bytes 196612
  25.2 10.7 %collective-permute-start.13 = (f32[8,512]{1,0:T(8,128)S(1)}, f32[8,512]{1,0:T(8,128)S(1)}, u32[]{:S(2)}, u32[]{:S(2)}) collective-permute-start(f32[8,512]{1,0:T(8,128)S(1)} %get-tuple-element.55), channel_id=1, source_target_pairs={{16,0},{17,1},{18,2},{19,3},{20,4},{21,5},{22,6},{23,7},{24,8},{25... | collective-permute-start | bytes 49160 | tf_op jit(solution)/shard_map/ppermute | solution.py:924
  26.5 26.6 %collective-permute-start.2 = (f32[112,512]{1,0:T(8,128)S(1)}, f32[112,512]{1,0:T(8,128)S(1)}, u32[]{:S(2)}, u32[]{:S(2)}) collective-permute-start(f32[112,512]{1,0:T(8,128)S(1)} %get-tuple-element.34), channel_id=1, source_target_pairs={{8,0},{9,1},{10,2},{11,3},{12,4},{13,5},{14,6},{15,7},{0,8},{1,9},... | collective-permute-start | bytes 688136 | tf_op jit(solution)/shard_map/ppermute | solution.py:864
  29.8 19.6 %collective-permute-start.4 = (f32[88,512]{1,0:T(8,128)S(1)}, f32[88,512]{1,0:T(8,128)S(1)}, u32[]{:S(2)}, u32[]{:S(2)}) collective-permute-start(f32[88,512]{1,0:T(8,128)S(1)} %get-tuple-element.36), channel_id=1, source_target_pairs={{4,0},{5,1},{6,2},{7,3},{8,4},{9,5},{10,6},{11,7},{12,8},{13,9},{1... | collective-permute-start | bytes 540680 | tf_op jit(solution)/shard_map/ppermute | solution.py:864
  31.3 18.1 %collective-permute-start.3 = (f32[88,512]{1,0:T(8,128)S(1)}, f32[88,512]{1,0:T(8,128)S(1)}, u32[]{:S(2)}, u32[]{:S(2)}) collective-permute-start(f32[88,512]{1,0:T(8,128)S(1)} %get-tuple-element.35.own), channel_id=1, source_target_pairs={{12,0},{13,1},{14,2},{15,3},{0,4},{1,5},{2,6},{3,7},{4,8},{5,9},{6... | collective-permute-start | bytes 540680 | tf_op jit(solution)/shard_map/ppermute | solution.py:864
